TPU v7x, 32 devices: a whole 2x2x4 slice. The times are simulated.
32 devices in a mesh: ctx: 8 (over y, x, core), tp: 4 (over z).
Axes of the slice: x: 2, y: 2, z: 4, core: 2. Of those that a mesh axis runs over, the one named last changes fastest.
Arguments:
- span_rows: bfloat16 [2, 256, 3584], P(None, 'ctx'), may hold values from -6 to 6
- step_rows: bfloat16 [4, 32, 3584], P(None, 'ctx'), may hold values from -6 to 6
- lengths: int32 [2], replicated, may hold values from 513 to 768
- sample_prompt: int32 [32], P('ctx'), may hold values from 0 to 1
- norm_gain: float32 [3584], replicated, may hold values from 0.5 to 1.5
- query_weight: bfloat16 [3584, 3584], P('ctx', 'tp'), may hold values from -0.1875 to 0.1875
- key_weight: bfloat16 [3584, 512], P(None, 'tp'), may hold values from -0.1875 to 0.1875
- value_weight: bfloat16 [3584, 512], P(None, 'tp'), may hold values from -0.09375 to 0.09375
- query_bias: float32 [3584], P('tp'), may hold values from -16 to 16
- key_bias: float32 [512], P('tp'), may hold values from -16 to 16
- value_bias: float32 [512], P('tp'), may hold values from -3 to 3
- out_weight: bfloat16 [3584, 3584], P('tp', 'ctx'), may hold values from -0.25 to 0.25
- cache_keys: bfloat16 [2, 512, 512], P(None, 'ctx', 'tp'), may hold values from -12 to 12
- cache_values: bfloat16 [2, 512, 512], P(None, 'ctx', 'tp'), may hold values from -6 to 6
Outputs:
- span_out: bfloat16 [2, 256, 3584], P(None, 'ctx', 'tp')
- dec_out: bfloat16 [4, 32, 3584], P(None, 'ctx', 'tp')
All inputs are finite; a program needn't handle non-finite values.
Results may differ from a plain program's by a relative error of at most 0.012.
The roundings to bfloat16 on the way count: a program that leaves them out, or rounds other values in their place, can miss the bound.
Values may be sent and summed in bfloat16 or wider, within the bound.
No kernel may reach another device: no remote copies, remote signals or barrier semaphores. Data moves between devices by JAX's collectives and lax.ppermute only.
A program may use at most 128 MiB of HBM per device.

v0:
```python
import functools
import math

import jax
import jax.numpy as jnp
from jax import lax
from jax.experimental import pallas as pl
from jax.experimental.pallas import tpu as pltpu
from jax.sharding import PartitionSpec as P


HEADS = 28
KV_HEADS = 4
HEAD = 128


ROPE_BASE = 1000000.0
NORM_EPS = 1e-06
MASKED = -1e30


def norm_rows(inputs, norm_gain):
    widened = inputs.astype(jnp.float32)
    inverse = lax.rsqrt(jnp.mean(widened * widened, axis=-1, keepdims=True) + NORM_EPS)
    return (widened * inverse * norm_gain).astype(jnp.bfloat16)


def rotate(vectors, positions):
    width = vectors.shape[-1]
    half = width // 2
    exponent = jnp.arange(half, dtype=jnp.float32) * (2.0 / width)
    frequency = jnp.exp(exponent * -math.log(ROPE_BASE))
    angles = positions.astype(jnp.float32)[..., None, None] * frequency
    cosine = jnp.cos(angles)
    sine = jnp.sin(angles)
    first = vectors[..., :half]
    second = vectors[..., half:]
    return jnp.concatenate(
        [first * cosine - second * sine, second * cosine + first * sine], axis=-1
    )


def project(normed, weight, bias):
    return jnp.dot(normed, weight, preferred_element_type=jnp.float32) + bias


def key_positions(count, prefix_dev, span_dev, prefix_all):
    row_index = jnp.arange(count, dtype=jnp.int32)
    device = row_index // (prefix_dev + span_dev)
    offset = row_index % (prefix_dev + span_dev)
    return jnp.where(
        offset < prefix_dev,
        device * prefix_dev + offset,
        prefix_all + device * span_dev + offset - prefix_dev,
    )


def local_gathering(
    span_rows,
    step_rows,
    lengths,
    sample_prompt,
    norm_gain,
    query_weight,
    key_weight,
    value_weight,
    query_bias,
    key_bias,
    value_bias,
    out_weight,
    cache_keys,
    cache_values,
):
    cycle_size = lax.axis_size("ctx")
    cycle_place = lax.axis_index("ctx")
    prompt_count = span_rows.shape[0]
    span_dev = span_rows.shape[1]
    prefix_dev = cache_keys.shape[1]
    kv_local = key_weight.shape[1] // HEAD
    kv_group = HEADS // KV_HEADS
    heads_local = kv_local * kv_group
    prefix_all = prefix_dev * cycle_size
    factor = HEAD ** (-0.5)
    full_query = lax.all_gather(query_weight, "ctx", axis=0, tiled=True)
    normed = norm_rows(span_rows, norm_gain)
    span_places = prefix_all + cycle_place * span_dev + jnp.arange(span_dev, dtype=jnp.int32)
    grid_places = jnp.broadcast_to(span_places, (prompt_count, span_dev))
    queries = rotate(
        project(normed, full_query, query_bias).reshape(prompt_count, span_dev, heads_local, HEAD),
        grid_places,
    ).astype(jnp.bfloat16)
    new_keys = rotate(
        project(normed, key_weight, key_bias).reshape(prompt_count, span_dev, kv_local, HEAD),
        grid_places,
    ).astype(jnp.bfloat16)
    new_values = project(normed, value_weight, value_bias).astype(jnp.bfloat16)
    key_block = jnp.concatenate(
        [cache_keys, new_keys.reshape(prompt_count, span_dev, kv_local * HEAD)], axis=1
    )
    value_block = jnp.concatenate([cache_values, new_values], axis=1)
    query_rows = (
        queries.reshape(prompt_count, span_dev, kv_local, kv_group, HEAD)
        .transpose(0, 2, 1, 3, 4)
        .reshape(prompt_count, kv_local, span_dev * kv_group, HEAD)
    )
    query_places = jnp.repeat(span_places, kv_group)
    row_count = span_dev * kv_group
    highest = jnp.full((prompt_count, kv_local, row_count), MASKED, jnp.float32)
    key_piece = lax.all_gather(key_block, "ctx", axis=1, tiled=True)
    value_piece = lax.all_gather(value_block, "ctx", axis=1, tiled=True)
    count = key_piece.shape[1]
    places = key_positions(count, prefix_dev, span_dev, prefix_all)
    key_grid = key_piece.reshape(prompt_count, count, kv_local, HEAD)
    value_grid = value_piece.reshape(prompt_count, count, kv_local, HEAD)
    scores = (
        jnp.einsum("pgqd,pkgd->pgqk", query_rows, key_grid, preferred_element_type=jnp.float32)
        * factor
    )
    visible = (places[None, None, None, :] < lengths[:, None, None, None]) & (
        places[None, None, None, :] <= query_places[None, None, :, None]
    )
    scores = jnp.where(visible, scores, MASKED)
    raised = jnp.maximum(highest, jnp.max(scores, axis=-1))
    weights = jnp.where(visible, jnp.exp(scores - raised[..., None]), 0.0)
    totals = jnp.sum(weights, axis=-1)
    blended = jnp.einsum(
        "pgqk,pkgd->pgqd",
        weights.astype(jnp.bfloat16),
        value_grid,
        preferred_element_type=jnp.float32,
    )
    highest, totals, blended = (raised, totals, blended)
    key_all, value_all = (
        lax.all_gather(key_block, "ctx", axis=1, tiled=True),
        lax.all_gather(value_block, "ctx", axis=1, tiled=True),
    )
    span_attention = (blended / totals[..., None]).astype(jnp.bfloat16)
    span_attention = (
        span_attention.reshape(prompt_count, kv_local, span_dev, kv_group, HEAD)
        .transpose(0, 2, 1, 3, 4)
        .reshape(prompt_count, span_dev, heads_local * HEAD)
    )
    full_out = lax.all_gather(out_weight, "ctx", axis=1, tiled=True)
    span_terms = jnp.dot(span_attention, full_out, preferred_element_type=jnp.float32)
    span_out = lax.psum_scatter(
        span_terms.astype(jnp.bfloat16), "tp", scatter_dimension=2, tiled=True
    )
    gathered_rows = key_all.shape[1]
    key_grid = key_all.reshape(prompt_count, gathered_rows, kv_local, HEAD)
    value_grid = value_all.reshape(prompt_count, gathered_rows, kv_local, HEAD)
    all_places = key_positions(gathered_rows, prefix_dev, span_dev, prefix_all)
    picked = sample_prompt[:, None] == jnp.arange(prompt_count, dtype=jnp.int32)[None, :]
    length_of = jnp.sum(jnp.where(picked, lengths[None, :], 0), axis=1)
    prefix_visible = picked[:, :, None] & (all_places[None, None, :] < length_of[:, None, None])
    wide_visible = prefix_visible[:, None, None, :, :]
    sample_count = step_rows.shape[1]
    step_count = step_rows.shape[0]
    step_ids = jnp.arange(step_count, dtype=jnp.int32)
    made_keys = jnp.zeros((sample_count, step_count, kv_local, HEAD), jnp.bfloat16)
    made_values = jnp.zeros((sample_count, step_count, kv_local, HEAD), jnp.bfloat16)
    outputs = []
    for step_index in range(step_count):
        normed_step = norm_rows(step_rows[step_index], norm_gain)
        places_now = length_of + step_index
        step_queries = rotate(
            project(normed_step, full_query, query_bias).reshape(sample_count, heads_local, HEAD),
            places_now,
        ).astype(jnp.bfloat16)
        step_queries = step_queries.reshape(sample_count, kv_local, kv_group, HEAD)
        fresh_keys = rotate(
            project(normed_step, key_weight, key_bias).reshape(sample_count, kv_local, HEAD),
            places_now,
        ).astype(jnp.bfloat16)
        fresh_values = (
            project(normed_step, value_weight, value_bias)
            .astype(jnp.bfloat16)
            .reshape(sample_count, kv_local, HEAD)
        )
        made_keys = made_keys.at[:, step_index].set(fresh_keys)
        made_values = made_values.at[:, step_index].set(fresh_values)
        own_visible = step_ids <= step_index
        far_scores = (
            jnp.einsum(
                "sgqd,pkgd->sgqpk", step_queries, key_grid, preferred_element_type=jnp.float32
            )
            * factor
        )
        far_scores = jnp.where(wide_visible, far_scores, MASKED)
        near_scores = (
            jnp.einsum(
                "sgqd,stgd->sgqt", step_queries, made_keys, preferred_element_type=jnp.float32
            )
            * factor
        )
        near_scores = jnp.where(own_visible, near_scores, MASKED)
        highest_now = jnp.maximum(jnp.max(far_scores, axis=(3, 4)), jnp.max(near_scores, axis=-1))
        far_weights = jnp.where(
            wide_visible, jnp.exp(far_scores - highest_now[..., None, None]), 0.0
        )
        near_weights = jnp.where(own_visible, jnp.exp(near_scores - highest_now[..., None]), 0.0)
        totals_now = jnp.sum(far_weights, axis=(3, 4)) + jnp.sum(near_weights, axis=-1)
        blended_now = jnp.einsum(
            "sgqpk,pkgd->sgqd",
            far_weights.astype(jnp.bfloat16),
            value_grid,
            preferred_element_type=jnp.float32,
        )
        blended_now = blended_now + jnp.einsum(
            "sgqt,stgd->sgqd",
            near_weights.astype(jnp.bfloat16),
            made_values,
            preferred_element_type=jnp.float32,
        )
        step_attention = (
            (blended_now / totals_now[..., None])
            .astype(jnp.bfloat16)
            .reshape(sample_count, heads_local * HEAD)
        )
        outputs.append(step_attention)
    stacked = jnp.stack(outputs)
    decode_terms = jnp.dot(stacked, full_out, preferred_element_type=jnp.float32)
    dec_out = lax.psum_scatter(
        decode_terms.astype(jnp.bfloat16), "tp", scatter_dimension=2, tiled=True
    )
    return (span_out, dec_out)


LOG2_E = 1.4426950408889634
VMEM = pl.BlockSpec(memory_space=pltpu.VMEM)
HBM = pl.BlockSpec(memory_space=pltpu.HBM)
SMEM = pl.BlockSpec(memory_space=pltpu.SMEM)
KERNEL = pltpu.CompilerParams(vmem_limit_bytes=16 * 2**20)
NORM_KERNEL = pltpu.CompilerParams(vmem_limit_bytes=66400000)
KEY_VALUE_KERNEL = pltpu.CompilerParams(vmem_limit_bytes=60 * 2**20)


def rotation_tables(positions):
    half = HEAD // 2
    lane = lax.broadcasted_iota(jnp.int32, (1, HEAD), 1)
    exponent = lax.rem(lane, half).astype(jnp.float32) * (2.0 / HEAD)
    frequency = jnp.exp(exponent * -math.log(ROPE_BASE))
    angles = positions.astype(jnp.float32) * frequency
    sine = jnp.sin(angles)
    return jnp.cos(angles), jnp.where(lane < half, -sine, sine)


def rotate_block(block, cosine, sine):
    return block * cosine + pltpu.roll(block, HEAD // 2, 1) * sine


def fetch_all(sources, targets, semaphores):
    copies = [
        pltpu.make_async_copy(source, target, semaphores.at[index])
        for index, (source, target) in enumerate(zip(sources, targets))
    ]
    for copy in copies:
        copy.start()
    for copy in copies:
        copy.wait()


def norm_kernel(place_ref, span_hbm, step_hbm, gain_hbm, *rest):
    *message_refs, normed_ref, widened, span_ref, step_ref, gain_ref, semaphores = rest
    fetch_all((span_hbm, step_hbm, gain_hbm), (span_ref, step_ref, gain_ref), semaphores)
    prompts, span_dev, _ = span_ref.shape
    steps, samples, _ = step_ref.shape
    for prompt in range(prompts):
        widened[prompt * span_dev : (prompt + 1) * span_dev, :] = span_ref[prompt].astype(
            jnp.float32
        )
    base = prompts * span_dev
    for step in range(steps):
        widened[base + step * samples : base + (step + 1) * samples, :] = step_ref[step].astype(
            jnp.float32
        )
    rows = widened[...]
    inverse = lax.rsqrt(jnp.mean(rows * rows, axis=-1, keepdims=True) + NORM_EPS)
    normed_ref[...] = (rows * inverse * gain_ref[...][None, :]).astype(jnp.bfloat16)
    width = message_refs[0].shape[1]
    for slot, message_ref in enumerate(message_refs):
        start = pl.multiple_of((place_ref[0] ^ slot) * width, width)
        message_ref[...] = normed_ref[:, pl.ds(start, width)]


def key_value_kernel(
    steps,
    ctx_ref,
    lengths_ref,
    sample_prompt_ref,
    *rest,
):
    chips = len(rest) - 16
    message_refs, rest = rest[:chips], rest[chips:]
    (key_weight_hbm, value_weight_hbm, *other_hbm), rest = rest[:6], rest[6:]
    (packed_ref, own_ref, cosine_ref, sine_ref), rest = rest[:4], rest[4:]
    weight_ref, *fetched, semaphores = rest
    key_bias_ref, value_bias_ref, cache_keys_ref, cache_values_ref = fetched[:4]
    prompts, prefix_dev, width = cache_keys_ref.shape
    copies = [
        pltpu.make_async_copy(source, target, semaphores.at[index])
        for index, (source, target) in enumerate(
            [
                (key_weight_hbm, weight_ref.at[:, :width]),
                (value_weight_hbm, weight_ref.at[:, width:]),
            ]
            + list(zip(other_hbm, fetched))
        )
    ]
    for copy in copies:
        copy.start()
    samples = sample_prompt_ref.shape[0]
    own_rows = steps * samples
    row_count, chip_width = message_refs[0].shape
    span_dev = (row_count - own_rows) // prompts
    block = prefix_dev + span_dev
    row_index = lax.broadcasted_iota(jnp.int32, (row_count, 1), 0)
    span_start = (2 * chips * prefix_dev) + ctx_ref[0] * span_dev
    positions = span_start + lax.rem(row_index, span_dev)
    own_index = row_index - prompts * span_dev
    for index in range(samples):
        start = lengths_ref[sample_prompt_ref[index]]
        taken = (own_index >= 0) & (lax.rem(own_index, samples) == index)
        positions = jnp.where(taken, start + lax.div(own_index, samples), positions)
    cosine, sine = rotation_tables(positions)
    cosine_ref[...], sine_ref[...] = cosine, sine
    for copy in copies:
        copy.wait()
    products = None
    for slot, message_ref in enumerate(message_refs):
        start = pl.multiple_of((lax.div(ctx_ref[0], 2) ^ slot) * chip_width, chip_width)
        product = jnp.dot(
            message_ref[...],
            weight_ref[pl.ds(start, chip_width), :],
            preferred_element_type=jnp.float32,
        )
        products = product if products is None else products + product
    keys = products[:, :width] + key_bias_ref[...][None, :]
    values = (products[:, width:] + value_bias_ref[...][None, :]).astype(jnp.bfloat16)
    keys = jnp.concatenate(
        [
            rotate_block(keys[:, at : at + HEAD], cosine, sine)
            for at in range(0, width, HEAD)
        ],
        axis=1,
    ).astype(jnp.bfloat16)
    for kind, (cache_ref, fresh) in enumerate(
        ((cache_keys_ref, keys), (cache_values_ref, values))
    ):
        for prompt in range(prompts):
            start = (kind * prompts + prompt) * block
            packed_ref[start : start + prefix_dev, :] = cache_ref[prompt]
            packed_ref[start + prefix_dev : start + block, :] = fresh[
                prompt * span_dev : (prompt + 1) * span_dev
            ]
        own_ref[kind] = fresh[prompts * span_dev :]


def query_kernel(core_ref, rows_ref, own_ref, other_ref, out_ref):
    half = own_ref.shape[0]

    def product(first_ref, second_ref):
        total = jnp.dot(rows_ref[:, :half], first_ref[...], preferred_element_type=jnp.float32)
        total = total + jnp.dot(
            rows_ref[:, half:], second_ref[...], preferred_element_type=jnp.float32
        )
        out_ref[...] = total.astype(out_ref.dtype)

    @pl.when(core_ref[0] == 0)
    def _():
        product(own_ref, other_ref)

    @pl.when(core_ref[0] == 1)
    def _():
        product(other_ref, own_ref)


def out_kernel(core_ref, rows_ref, own_ref, other_ref, out_ref):
    half = own_ref.shape[0]
    rows = rows_ref[...]

    def product(weight_ref):
        return lax.dot_general(
            rows, weight_ref[...], (((1,), (1,)), ((), ())), preferred_element_type=jnp.float32
        ).astype(out_ref.dtype)

    @pl.when(core_ref[0] == 0)
    def _():
        out_ref[:, :half] = product(own_ref)
        out_ref[:, half:] = product(other_ref)

    @pl.when(core_ref[0] == 1)
    def _():
        out_ref[:, :half] = product(other_ref)
        out_ref[:, half:] = product(own_ref)


def attend_kernel(
    steps,
    prefix_dev,
    ctx_ref,
    lengths_ref,
    sample_prompt_ref,
    bias_ref,
    cosine_ref,
    sine_ref,
    own_ref,
    *rest,
):
    *query_refs, near_ref, far_ref, out_ref, rotated = rest
    packed_refs = (near_ref, far_ref)
    prompts = lengths_ref.shape[0]
    samples = sample_prompt_ref.shape[0]
    own_rows = steps * samples
    row_count, columns = out_ref.shape
    span_dev = (row_count - own_rows) // prompts
    kv_width = own_ref.shape[2]
    kv_local = kv_width // HEAD
    heads_local = columns // HEAD
    group = heads_local // kv_local
    scale = HEAD ** (-0.5) * LOG2_E
    cosine, sine = cosine_ref[...], sine_ref[...]
    for head in range(heads_local):
        span = slice(head * HEAD, (head + 1) * HEAD)
        total = query_refs[0][:, span].astype(jnp.float32)
        for query_ref in query_refs[1:]:
            total = total + query_ref[:, span].astype(jnp.float32)
        total = total + bias_ref[span][None, :]
        rotated[:, span] = rotate_block(total, cosine, sine).astype(jnp.bfloat16)
    chips, packed_rows, _ = near_ref.shape
    block = packed_rows // (2 * prompts)
    prefix_all = 2 * chips * prefix_dev
    key_index = lax.broadcasted_iota(jnp.int32, (1, 2 * chips * block), 1)
    slot, offset = lax.div(key_index, block), lax.rem(key_index, block)
    owner = ctx_ref[0] ^ (2 * lax.rem(slot, chips) + lax.div(slot, chips))
    places = jnp.where(
        offset < prefix_dev,
        owner * prefix_dev + offset,
        prefix_all + owner * span_dev + offset - prefix_dev,
    )

    def rows_of(start, count, first_head):
        return jnp.concatenate(
            [
                rotated[start : start + count, head * HEAD : (head + 1) * HEAD]
                for head in range(first_head, first_head + group)
            ],
            axis=0,
        )

    def cached(kind, prompt, group_index):
        start = (kind * prompts + prompt) * block
        lanes = slice(group_index * HEAD, (group_index + 1) * HEAD)
        return jnp.concatenate(
            [
                packed_ref[index, start : start + block, lanes]
                for packed_ref in packed_refs
                for index in range(packed_ref.shape[0])
            ],
            axis=0,
        )

    def score(queries, keys, visible):
        raw = lax.dot_general(
            queries, keys, (((1,), (1,)), ((), ())), preferred_element_type=jnp.float32
        )
        return jnp.where(visible, raw * scale, MASKED)

    def store(start, count, first_head, blended):
        for offset in range(group):
            head = first_head + offset
            out_ref[start : start + count, head * HEAD : (head + 1) * HEAD] = blended[
                offset * count : (offset + 1) * count
            ]

    for group_index in range(kv_local):
        first_head = group_index * group
        keys = [cached(0, prompt, group_index) for prompt in range(prompts)]
        values = [cached(1, prompt, group_index) for prompt in range(prompts)]
        row_index = lax.broadcasted_iota(jnp.int32, (group * span_dev, 1), 0)
        query_places = prefix_all + ctx_ref[0] * span_dev + lax.rem(row_index, span_dev)
        for prompt in range(prompts):
            queries = rows_of(prompt * span_dev, span_dev, first_head)
            limit = jnp.minimum(query_places, lengths_ref[prompt] - 1)
            scores = score(queries, keys[prompt], places <= limit)
            highest = jnp.max(scores, axis=-1, keepdims=True)
            weights = jnp.exp2(scores - highest)
            totals = jnp.sum(weights, axis=-1, keepdims=True)
            blended = jnp.dot(
                weights.astype(jnp.bfloat16), values[prompt], preferred_element_type=jnp.float32
            )
            store(
                prompt * span_dev, span_dev, first_head, (blended / totals).astype(jnp.bfloat16)
            )
        start = prompts * span_dev
        queries = rows_of(start, own_rows, first_head)
        row_index = lax.rem(lax.broadcasted_iota(jnp.int32, (group * own_rows, 1), 0), own_rows)
        sample = lax.rem(row_index, samples)
        step = lax.div(row_index, samples)
        own_index = lax.broadcasted_iota(jnp.int32, (1, own_rows), 1)
        own_visible = (lax.rem(own_index, samples) == sample) & (
            lax.div(own_index, samples) <= step
        )
        own_lanes = slice(group_index * HEAD, (group_index + 1) * HEAD)
        parts = [score(queries, own_ref[0, :, own_lanes], own_visible)]
        for prompt in range(prompts):
            limit = jnp.full(row_index.shape, -1, jnp.int32)
            for index in range(samples):
                reach = jnp.where(
                    sample_prompt_ref[index] == prompt, lengths_ref[prompt] - 1, -1
                )
                limit = jnp.where(sample == index, reach, limit)
            parts.append(score(queries, keys[prompt], places <= limit))
        highest = functools.reduce(
            jnp.maximum, [jnp.max(part, axis=-1, keepdims=True) for part in parts]
        )
        weights = [jnp.exp2(part - highest) for part in parts]
        totals = sum(jnp.sum(weight, axis=-1, keepdims=True) for weight in weights)
        blended = sum(
            jnp.dot(weight.astype(jnp.bfloat16), value, preferred_element_type=jnp.float32)
            for weight, value in zip(weights, [own_ref[1, :, own_lanes]] + values)
        )
        store(start, own_rows, first_head, (blended / totals).astype(jnp.bfloat16))


def add_kernel(*refs):
    share_refs, span_ref, step_ref = refs[:-2], refs[-2], refs[-1]
    prompts, span_dev, _ = span_ref.shape
    steps, samples, _ = step_ref.shape
    total = share_refs[0][...].astype(jnp.float32)
    for share_ref in share_refs[1:]:
        total = total + share_ref[...].astype(jnp.float32)
    for prompt in range(prompts):
        rows = slice(prompt * span_dev, (prompt + 1) * span_dev)
        span_ref[prompt] = total[rows].astype(jnp.bfloat16)
    for step in range(steps):
        start = prompts * span_dev + step * samples
        step_ref[step] = total[start : start + samples].astype(jnp.bfloat16)


def local_moving_rows(
    span_rows,
    step_rows,
    lengths,
    sample_prompt,
    norm_gain,
    query_weight,
    key_weight,
    value_weight,
    query_bias,
    key_bias,
    value_bias,
    out_weight,
    cache_keys,
    cache_values,
):
    ctx_size = lax.axis_size("ctx")
    tp_size = lax.axis_size("tp")
    ctx_place = lax.axis_index("ctx")
    tp_place = lax.axis_index("tp")
    chip_place, core_place = ctx_place // 2, ctx_place % 2
    chips = ctx_size // 2
    prompts, span_dev, model = span_rows.shape
    steps, samples, _ = step_rows.shape
    prefix_dev, kv_width = cache_keys.shape[1:]
    columns = query_weight.shape[1]
    row_count = prompts * span_dev + steps * samples
    chip_width = model // chips
    core_pairs = [(place, place ^ 1) for place in range(ctx_size)]

    def to_chip(block, slot):
        return lax.ppermute(
            block, "ctx", [(place, place ^ (2 * slot)) for place in range(ctx_size)]
        )

    bf16 = functools.partial(jax.ShapeDtypeStruct, dtype=jnp.bfloat16)
    messages = pl.pallas_call(
        norm_kernel,
        out_shape=[bf16((row_count, chip_width))] * chips,
        in_specs=[SMEM, HBM, HBM, HBM],
        out_specs=[VMEM] * chips,
        scratch_shapes=[
            pltpu.VMEM((row_count, model), jnp.bfloat16),
            pltpu.VMEM((row_count, model), jnp.float32),
            pltpu.VMEM(span_rows.shape, jnp.bfloat16),
            pltpu.VMEM(step_rows.shape, jnp.bfloat16),
            pltpu.VMEM(norm_gain.shape, jnp.float32),
            pltpu.SemaphoreType.DMA((3,)),
        ],
        compiler_params=NORM_KERNEL,
        name="norm",
    )(chip_place.reshape(1), span_rows, step_rows, norm_gain)
    inbound = [messages[0]] + [to_chip(messages[slot], slot) for slot in range(1, chips)]
    other_query = lax.ppermute(query_weight, "ctx", core_pairs)
    other_out = lax.ppermute(out_weight.T, "ctx", core_pairs)
    block = prefix_dev + span_dev
    table = jax.ShapeDtypeStruct((row_count, HEAD), jnp.float32)
    packed, own, cosine, sine = pl.pallas_call(
        functools.partial(key_value_kernel, steps),
        out_shape=[
            bf16((2 * prompts * block, kv_width)),
            bf16((2, steps * samples, kv_width)),
            table,
            table,
        ],
        in_specs=[SMEM] * 3 + [VMEM] * chips + [HBM] * 6,
        out_specs=[VMEM] * 4,
        scratch_shapes=[pltpu.VMEM((model, 2 * kv_width), jnp.bfloat16)]
        + [
            pltpu.VMEM(array.shape, array.dtype)
            for array in (key_bias, value_bias, cache_keys, cache_values)
        ]
        + [pltpu.SemaphoreType.DMA((6,))],
        compiler_params=KEY_VALUE_KERNEL,
        name="key_value",
    )(
        ctx_place.reshape(1),
        lengths,
        sample_prompt,
        *messages,
        key_weight,
        value_weight,
        key_bias,
        value_bias,
        cache_keys,
        cache_values,
    )
    near_packed = jnp.stack([packed] + [to_chip(packed, slot) for slot in range(1, chips)])
    far_packed = lax.ppermute(near_packed, "ctx", core_pairs)

    shares = []
    for slot, rows in enumerate(inbound):
        partial = pl.pallas_call(
            query_kernel,
            out_shape=jax.ShapeDtypeStruct(
                (row_count, columns), jnp.bfloat16 if slot else jnp.float32
            ),
            in_specs=[SMEM] + [VMEM] * 3,
            out_specs=VMEM,
            compiler_params=KERNEL,
            name="query_dot",
        )(core_place.reshape(1), rows, query_weight, other_query)
        if slot:
            partial = to_chip(partial, slot)
        shares.append(partial)

    attention = pl.pallas_call(
        functools.partial(attend_kernel, steps, prefix_dev),
        out_shape=bf16((row_count, columns)),
        in_specs=[SMEM] * 3 + [VMEM] * (4 + chips + 2),
        out_specs=VMEM,
        scratch_shapes=[pltpu.VMEM((row_count, columns), jnp.bfloat16)],
        compiler_params=KERNEL,
        name="attend",
    )(
        ctx_place.reshape(1),
        lengths,
        sample_prompt,
        query_bias,
        cosine,
        sine,
        own,
        *shares,
        near_packed,
        far_packed,
    )

    attended = [attention] + [to_chip(attention, slot) for slot in range(1, chips)]
    returned = []
    for slot, rows in enumerate(attended):
        terms = pl.pallas_call(
            out_kernel,
            out_shape=bf16((row_count, columns)),
            in_specs=[SMEM] + [VMEM] * 3,
            out_specs=VMEM,
            compiler_params=KERNEL,
            name="out_dot",
        )(core_place.reshape(1), rows, out_weight.T, other_out)
        if slot:
            terms = to_chip(terms, slot)
        returned.append(terms)
    returned = jnp.stack(returned)

    def columns_of(slot):
        return lax.dynamic_index_in_dim(returned, tp_place ^ slot ^ chip_place, 0, keepdims=False)

    finals = [columns_of(0)]
    for slot in range(1, tp_size):
        finals.append(
            lax.ppermute(
                columns_of(slot), "tp", [(place, place ^ slot) for place in range(tp_size)]
            )
        )
    return pl.pallas_call(
        add_kernel,
        out_shape=[bf16((prompts, span_dev, columns)), bf16((steps, samples, columns))],
        in_specs=[VMEM] * tp_size,
        out_specs=[VMEM] * 2,
        compiler_params=KERNEL,
        name="add",
    )(*finals)


def rows_are_lighter(mesh, rows, model):
    ctx_size, tp_size = mesh.shape["ctx"], mesh.shape["tp"]
    fits = ctx_size == 2 * tp_size and tp_size & (tp_size - 1) == 0
    return fits and rows < model


def solution(mesh):
    def local(span_rows, step_rows, lengths, sample_prompt, norm_gain, query_weight, *others):
        whole_rows = (span_rows.shape[0] * span_rows.shape[1], step_rows.shape[0] * step_rows.shape[1])
        rows = sum(whole_rows) * mesh.shape["ctx"]
        form = local_gathering
        if rows_are_lighter(mesh, rows, query_weight.shape[0] * mesh.shape["ctx"]):
            form = local_moving_rows
        return form(
            span_rows, step_rows, lengths, sample_prompt, norm_gain, query_weight, *others
        )

    return jax.shard_map(
        local,
        mesh=mesh,
        in_specs=(
            P(None, "ctx", None),
            P(None, "ctx", None),
            P(),
            P("ctx"),
            P(),
            P("ctx", "tp"),
            P(None, "tp"),
            P(None, "tp"),
            P("tp"),
            P("tp"),
            P("tp"),
            P("tp", "ctx"),
            P(None, "ctx", "tp"),
            P(None, "ctx", "tp"),
        ),
        out_specs=(P(None, "ctx", "tp"), P(None, "ctx", "tp")),
        check_vma=False,
    )
```

profile of v0, /device:TPU:0, one launch (start us, length us, event | category | flops | bytes accessed | tf_op | source)
XLA Modules:
  0.0 72.3 jit_solution(11687796372421081737)
XLA Ops:
  0.6 0.6 collective-permute-start
  1.2 0.1 collective-permute-start.11
  1.3 2.2 %norm.1 = (bf16[80,896]{1,0:T(8,128)(2,1)}, bf16[80,896]{1,0:T(8,128)(2,1)}, bf16[80,896]{1,0:T(8,128)(2,1)}, bf16[80,896]{1,0:T(8,128)(2,1)}) custom-call(s32[1]{0:T(128)} %bitcast.2.place_ref, bf16[2,32,3584]{2,1,0:T(8,128)(2,1)} %span_hbm.1, bf16[4,4,3584]{2,1,0:T(4,128)(2,1)} %step_hbm.1, f32[3584]{0:T(1024)} %gain_hbm.1), custom_call_target="tpu_custom_call" | custom-call | tf_op jit(solution)/shard_map/norm/pallas_call | solution.py:576
  3.5 0.0 copy-start.11
  3.5 0.0 copy-start.10
  3.6 3.9 %key_value.1 = (bf16[384,128]{1,0:T(8,128)(2,1)}, bf16[2,16,128]{2,1,0:T(8,128)(2,1)}, f32[80,128]{1,0:T(8,128)}, f32[80,128]{1,0:T(8,128)}) custom-call(s32[1]{0:T(128)} %bitcast.1.ctx_ref, s32[2]{0:T(128)} %lengths_ref.3, s32[4]{0:T(128)} %sample_prompt_ref.3, bf16[80,896]{1,0:T(8,128)(2,1)} %get-tuple-element.10.rest_0_.rows_ref, ...), custom_call_target="tpu_custom_call" | custom-call | tf_op jit(solution)/shard_map/key_value/pallas_call | solution.py:597
  7.4 0.0 copy-start
  7.5 3.9 %collective-permute-start.9 = (bf16[384,128]{1,0:T(8,128)(2,1)}, bf16[384,128]{1,0:T(8,128)(2,1)S(1)}, u32[]{:S(2)}, u32[]{:S(2)}) collective-permute-start(bf16[384,128]{1,0:T(8,128)(2,1)} %get-tuple-element.17), channel_id=1, source_target_pairs={{0,24},{4,28},{8,16},{12,20},{16,8},{20,12},{24,0},{28,4},{1,25},{... | collective-permute-start | bytes 294920 | tf_op jit(solution)/shard_map/ppermute | solution.py:571
  11.4 0.5 collective-permute-start.8
  11.9 0.1 collective-permute-start.7
  12.0 2.9 %collective-permute-done.9 = bf16[384,128]{1,0:T(8,128)(2,1)S(1)} collective-permute-done((bf16[384,128]{1,0:T(8,128)(2,1)}, bf16[384,128]{1,0:T(8,128)(2,1)S(1)}, u32[]{:S(2)}, u32[]{:S(2)}) %collective-permute-start.9) | collective-permute-done | bytes 98336 | tf_op jit(solution)/shard_map/ppermute | solution.py:571
  14.9 2.0 %collective-permute-start.1 = (bf16[80,896]{1,0:T(8,128)(2,1)S(1)}, bf16[80,896]{1,0:T(8,128)(2,1)S(1)}, u32[]{:S(2)}, u32[]{:S(2)}) collective-permute-start(bf16[80,896]{1,0:T(8,128)(2,1)S(1)} %copy-done.11), channel_id=1, source_target_pairs={{0,8},{4,12},{8,0},{12,4},{16,24},{20,28},{24,16},{28,20},{1,9},{5... | collective-permute-start | bytes 430088 | tf_op jit(solution)/shard_map/ppermute | solution.py:571
  16.9 0.0 collective-permute-done.8
  16.9 0.3 collective-permute-done.7
  17.2 0.9 %pad_maximum_fusion.1.rest_4_ = bf16[4,384,128]{2,1,0:T(8,128)(2,1)S(1)} fusion(bf16[1,384,128]{2,1,0:T(8,128)(2,1)S(1)} %bitcast.30, bf16[1,384,128]{2,1,0:T(8,128)(2,1)S(1)} %bitcast.31, bf16[1,384,128]{2,1,0:T(8,128)(2,1)S(1)} %bitcast.32, bf16[1,384,128]{2,1,0:T(8,128)(2,1)} %bitcast.29), kind=kLoop, calls=%fused_computation.1 | loop fusion | flops 589824 | bytes 786432 | tf_op jit(solution)/shard_map/stack | solution.py:627
  18.2 0.1 collective-permute-start.10
  18.3 1.6 %collective-permute-start.3 = (bf16[80,896]{1,0:T(8,128)(2,1)S(1)}, bf16[80,896]{1,0:T(8,128)(2,1)S(1)}, u32[]{:S(2)}, u32[]{:S(2)}) collective-permute-start(bf16[80,896]{1,0:T(8,128)(2,1)S(1)} %copy-done.10), channel_id=1, source_target_pairs={{0,16},{4,20},{8,24},{12,28},{16,0},{20,4},{24,8},{28,12},{1,17},{... | collective-permute-start | bytes 430088 | tf_op jit(solution)/shard_map/ppermute | solution.py:571
  19.9 0.2 collective-permute-done.1.rows_ref
  20.1 3.2 %collective-permute-start.5 = (bf16[80,896]{1,0:T(8,128)(2,1)S(1)}, bf16[80,896]{1,0:T(8,128)(2,1)S(1)}, u32[]{:S(2)}, u32[]{:S(2)}) collective-permute-start(bf16[80,896]{1,0:T(8,128)(2,1)S(1)} %copy-done.9), channel_id=1, source_target_pairs={{0,24},{4,28},{8,16},{12,20},{16,8},{20,12},{24,0},{28,4},{1,25},{... | collective-permute-start | bytes 430088 | tf_op jit(solution)/shard_map/ppermute | solution.py:571
  23.3 0.0 collective-permute-done.other_ref
  23.3 1.6 %query_dot.5 = bf16[80,896]{1,0:T(8,128)(2,1)S(1)} custom-call(s32[1]{0:T(128)} %bitcast.core_ref, bf16[80,896]{1,0:T(8,128)(2,1)S(1)} %collective-permute-done.1.rows_ref, bf16[448,896]{1,0:T(8,128)(2,1)S(1)} %copy-done, bf16[448,896]{1,0:T(8,128)(2,1)} %collective-permute-done.other_ref), custom_call_target="tpu_custom_call" | custom-call | tf_op jit(solution)/shard_map/query_dot/pallas_call | solution.py:632
  24.9 0.3 collective-permute-start.2
  25.2 1.9 %collective-permute-done.3.rows_ref = bf16[80,896]{1,0:T(8,128)(2,1)S(1)} collective-permute-done((bf16[80,896]{1,0:T(8,128)(2,1)S(1)}, bf16[80,896]{1,0:T(8,128)(2,1)S(1)}, u32[]{:S(2)}, u32[]{:S(2)}) %collective-permute-start.3) | collective-permute-done | bytes 143392 | tf_op jit(solution)/shard_map/ppermute | solution.py:571
  27.1 1.6 %query_dot.6 = bf16[80,896]{1,0:T(8,128)(2,1)S(1)} custom-call(s32[1]{0:T(128)} %bitcast.core_ref, bf16[80,896]{1,0:T(8,128)(2,1)S(1)} %collective-permute-done.3.rows_ref, bf16[448,896]{1,0:T(8,128)(2,1)S(1)} %copy-done, bf16[448,896]{1,0:T(8,128)(2,1)} %collective-permute-done.other_ref), custom_call_target="tpu_custom_call" | custom-call | tf_op jit(solution)/shard_map/query_dot/pallas_call | solution.py:632
  28.7 0.0 copy-start.2
  28.7 1.9 %collective-permute-start.4 = (bf16[80,896]{1,0:T(8,128)(2,1)S(1)}, bf16[80,896]{1,0:T(8,128)(2,1)S(1)}, u32[]{:S(2)}, u32[]{:S(2)}) collective-permute-start(bf16[80,896]{1,0:T(8,128)(2,1)S(1)} %query_dot.6), channel_id=1, source_target_pairs={{0,16},{4,20},{8,24},{12,28},{16,0},{20,4},{24,8},{28,12},{1,17},{... | collective-permute-start | bytes 430088 | tf_op jit(solution)/shard_map/ppermute | solution.py:571
  30.5 0.0 collective-permute-done.5.rows_ref
  30.5 1.6 %query_dot.7 = bf16[80,896]{1,0:T(8,128)(2,1)S(1)} custom-call(s32[1]{0:T(128)} %bitcast.core_ref, bf16[80,896]{1,0:T(8,128)(2,1)S(1)} %collective-permute-done.5.rows_ref, bf16[448,896]{1,0:T(8,128)(2,1)S(1)} %copy-done, bf16[448,896]{1,0:T(8,128)(2,1)} %collective-permute-done.other_ref), custom_call_target="tpu_custom_call" | custom-call | tf_op jit(solution)/shard_map/query_dot/pallas_call | solution.py:632
  32.1 1.8 %collective-permute-start.6 = (bf16[80,896]{1,0:T(8,128)(2,1)S(1)}, bf16[80,896]{1,0:T(8,128)(2,1)S(1)}, u32[]{:S(2)}, u32[]{:S(2)}) collective-permute-start(bf16[80,896]{1,0:T(8,128)(2,1)S(1)} %query_dot.7), channel_id=1, source_target_pairs={{0,24},{4,28},{8,16},{12,20},{16,8},{20,12},{24,0},{28,4},{1,25},{... | collective-permute-start | bytes 430088 | tf_op jit(solution)/shard_map/ppermute | solution.py:571
  33.9 1.6 %query_dot.4.rest_0_ = f32[80,896]{1,0:T(8,128)S(1)} custom-call(s32[1]{0:T(128)} %bitcast.core_ref, bf16[80,896]{1,0:T(8,128)(2,1)S(1)} %copy-done.2, bf16[448,896]{1,0:T(8,128)(2,1)S(1)} %copy-done, bf16[448,896]{1,0:T(8,128)(2,1)} %collective-permute-done.other_ref), custom_call_target="tpu_custom_call" | custom-call | tf_op jit(solution)/shard_map/query_dot/pallas_call | solution.py:632
  35.5 0.0 copy-start.6
  35.5 0.0 collective-permute-done.10.rest_5_
  35.5 0.0 collective-permute-done.2.rest_1_
  35.6 0.7 collective-permute-done.4.rest_2_
  36.3 1.9 %collective-permute-done.6.rest_3_ = bf16[80,896]{1,0:T(8,128)(2,1)S(1)} collective-permute-done((bf16[80,896]{1,0:T(8,128)(2,1)S(1)}, bf16[80,896]{1,0:T(8,128)(2,1)S(1)}, u32[]{:S(2)}, u32[]{:S(2)}) %collective-permute-start.6) | collective-permute-done | bytes 143392 | tf_op jit(solution)/shard_map/ppermute | solution.py:571
  38.2 0.6 copy-done.7
  38.8 0.0 copy-done.8
  38.9 2.1 %attend.1.rows_ref = bf16[80,896]{1,0:T(8,128)(2,1)S(1)} custom-call(s32[1]{0:T(128)} %bitcast.1.ctx_ref, s32[2]{0:T(128)S(1)} %copy-done.7, s32[4]{0:T(128)S(1)} %copy-done.8, f32[896]{0:T(1024)S(1)} %copy-done.6, f32[80,128]{1,0:T(8,128)S(1)} %copy-done.3, f32[80,128]{1,0:T(8,128)S(1)} %copy-done.4, bf16[2,16,128]{2,1,0:T(8,128)(2,1)S(1)} %copy-done.5, ...), custom_call_target="tpu_custom_call" | custom-call | tf_op jit(solution)/shard_map/attend/pallas_call | solution.py:646
  41.0 1.8 %collective-permute-start.16 = (bf16[80,896]{1,0:T(8,128)(2,1)S(1)}, bf16[80,896]{1,0:T(8,128)(2,1)S(1)}, u32[]{:S(2)}, u32[]{:S(2)}) collective-permute-start(bf16[80,896]{1,0:T(8,128)(2,1)S(1)} %attend.1.rows_ref), channel_id=1, source_target_pairs={{0,24},{4,28},{8,16},{12,20},{16,8},{20,12},{24,0},{28,4},{1,25},{... | collective-permute-start | bytes 430088 | tf_op jit(solution)/shard_map/ppermute | solution.py:571
  42.8 0.5 collective-permute-start.14
  43.3 1.2 %collective-permute-start.12 = (bf16[80,896]{1,0:T(8,128)(2,1)S(1)}, bf16[80,896]{1,0:T(8,128)(2,1)S(1)}, u32[]{:S(2)}, u32[]{:S(2)}) collective-permute-start(bf16[80,896]{1,0:T(8,128)(2,1)S(1)} %attend.1.rows_ref), channel_id=1, source_target_pairs={{0,8},{4,12},{8,0},{12,4},{16,24},{20,28},{24,16},{28,20},{1,9},{5... | collective-permute-start | bytes 430088 | tf_op jit(solution)/shard_map/ppermute | solution.py:571
  44.5 0.0 collective-permute-done.11.other_ref
  44.5 2.6 %collective-permute-done.16.rows_ref = bf16[80,896]{1,0:T(8,128)(2,1)S(1)} collective-permute-done((bf16[80,896]{1,0:T(8,128)(2,1)S(1)}, bf16[80,896]{1,0:T(8,128)(2,1)S(1)}, u32[]{:S(2)}, u32[]{:S(2)}) %collective-permute-start.16) | collective-permute-done | bytes 143392 | tf_op jit(solution)/shard_map/ppermute | solution.py:571
  47.1 1.8 %out_dot.7 = bf16[80,896]{1,0:T(8,128)(2,1)S(1)} custom-call(s32[1]{0:T(128)} %bitcast.core_ref, bf16[80,896]{1,0:T(8,128)(2,1)S(1)} %collective-permute-done.16.rows_ref, bf16[448,896]{1,0:T(8,128)(2,1)S(1)} %bitcast.21, bf16[448,896]{1,0:T(8,128)(2,1)} %collective-permute-done.11.other_ref), custom_call_target="tpu_custom_call" | custom-call | tf_op jit(solution)/shard_map/out_dot/pallas_call | solution.py:670
  48.9 1.8 %collective-permute-start.17 = (bf16[80,896]{1,0:T(8,128)(2,1)S(1)}, bf16[80,896]{1,0:T(8,128)(2,1)S(1)}, u32[]{:S(2)}, u32[]{:S(2)}) collective-permute-start(bf16[80,896]{1,0:T(8,128)(2,1)S(1)} %out_dot.7), channel_id=1, source_target_pairs={{0,24},{4,28},{8,16},{12,20},{16,8},{20,12},{24,0},{28,4},{1,25},{... | collective-permute-start | bytes 430088 | tf_op jit(solution)/shard_map/ppermute | solution.py:571
  50.8 0.0 collective-permute-done.14.rows_ref
  50.8 1.8 %out_dot.6 = bf16[80,896]{1,0:T(8,128)(2,1)S(1)} custom-call(s32[1]{0:T(128)} %bitcast.core_ref, bf16[80,896]{1,0:T(8,128)(2,1)S(1)} %collective-permute-done.14.rows_ref, bf16[448,896]{1,0:T(8,128)(2,1)S(1)} %bitcast.22, bf16[448,896]{1,0:T(8,128)(2,1)} %collective-permute-done.11.other_ref), custom_call_target="tpu_custom_call" | custom-call | tf_op jit(solution)/shard_map/out_dot/pallas_call | solution.py:670
  52.6 0.6 collective-permute-start.15
  53.2 0.0 collective-permute-done.12.rows_ref
  53.2 1.8 %out_dot.5 = bf16[80,896]{1,0:T(8,128)(2,1)S(1)} custom-call(s32[1]{0:T(128)} %bitcast.core_ref, bf16[80,896]{1,0:T(8,128)(2,1)S(1)} %collective-permute-done.12.rows_ref, bf16[448,896]{1,0:T(8,128)(2,1)S(1)} %bitcast.23, bf16[448,896]{1,0:T(8,128)(2,1)} %collective-permute-done.11.other_ref), custom_call_target="tpu_custom_call" | custom-call | tf_op jit(solution)/shard_map/out_dot/pallas_call | solution.py:670
  55.1 1.3 %collective-permute-start.13 = (bf16[80,896]{1,0:T(8,128)(2,1)S(1)}, bf16[80,896]{1,0:T(8,128)(2,1)S(1)}, u32[]{:S(2)}, u32[]{:S(2)}) collective-permute-start(bf16[80,896]{1,0:T(8,128)(2,1)S(1)} %out_dot.5), channel_id=1, source_target_pairs={{0,8},{4,12},{8,0},{12,4},{16,24},{20,28},{24,16},{28,20},{1,9},{5... | collective-permute-start | bytes 430088 | tf_op jit(solution)/shard_map/ppermute | solution.py:571
  56.3 1.8 %out_dot.4 = bf16[80,896]{1,0:T(8,128)(2,1)S(1)} custom-call(s32[1]{0:T(128)} %bitcast.core_ref, bf16[80,896]{1,0:T(8,128)(2,1)S(1)} %attend.1.rows_ref, bf16[448,896]{1,0:T(8,128)(2,1)S(1)} %bitcast.24, bf16[448,896]{1,0:T(8,128)(2,1)} %collective-permute-done.11.other_ref), custom_call_target="tpu_custom_call" | custom-call | tf_op jit(solution)/shard_map/out_dot/pallas_call | solution.py:670
  58.2 0.0 collective-permute-done.17
  58.2 0.0 collective-permute-done.15
  58.2 2.0 %collective-permute-done.13 = bf16[80,896]{1,0:T(8,128)(2,1)S(1)} collective-permute-done((bf16[80,896]{1,0:T(8,128)(2,1)S(1)}, bf16[80,896]{1,0:T(8,128)(2,1)S(1)}, u32[]{:S(2)}, u32[]{:S(2)}) %collective-permute-start.13) | collective-permute-done | bytes 143392 | tf_op jit(solution)/shard_map/ppermute | solution.py:571
  60.2 0.1 pad_maximum_fusion
  60.3 0.1 dynamic-slice_bitcast_fusion
  60.4 1.6 %collective-permute-start.18 = (bf16[80,896]{1,0:T(8,128)(2,1)S(1)}, bf16[80,896]{1,0:T(8,128)(2,1)S(1)}, u32[]{:S(2)}, u32[]{:S(2)}) collective-permute-start(bf16[80,896]{1,0:T(8,128)(2,1)S(1)} %get-tuple-element.20), channel_id=1, source_target_pairs={{0,1},{1,0},{2,3},{3,2},{4,5},{5,4},{6,7},{7,6},{8,9},{9,8},{10,11... | collective-permute-start | bytes 430088 | tf_op jit(solution)/shard_map/ppermute | solution.py:689
  62.0 2.6 %collective-permute-start.19 = (bf16[80,896]{1,0:T(8,128)(2,1)S(1)}, bf16[80,896]{1,0:T(8,128)(2,1)S(1)}, u32[]{:S(2)}, u32[]{:S(2)}) collective-permute-start(bf16[80,896]{1,0:T(8,128)(2,1)S(1)} %get-tuple-element.19), channel_id=1, source_target_pairs={{0,2},{1,3},{2,0},{3,1},{4,6},{5,7},{6,4},{7,5},{8,10},{9,11},{10,... | collective-permute-start | bytes 430088 | tf_op jit(solution)/shard_map/ppermute | solution.py:689
  64.6 0.2 collective-permute-start.20
  64.8 3.0 %collective-permute-done.18.refs_1_ = bf16[80,896]{1,0:T(8,128)(2,1)S(1)} collective-permute-done((bf16[80,896]{1,0:T(8,128)(2,1)S(1)}, bf16[80,896]{1,0:T(8,128)(2,1)S(1)}, u32[]{:S(2)}, u32[]{:S(2)}) %collective-permute-start.18) | collective-permute-done | bytes 143392 | tf_op jit(solution)/shard_map/ppermute | solution.py:689
  67.9 2.0 %collective-permute-done.19.refs_2_ = bf16[80,896]{1,0:T(8,128)(2,1)S(1)} collective-permute-done((bf16[80,896]{1,0:T(8,128)(2,1)S(1)}, bf16[80,896]{1,0:T(8,128)(2,1)S(1)}, u32[]{:S(2)}, u32[]{:S(2)}) %collective-permute-start.19) | collective-permute-done | bytes 143392 | tf_op jit(solution)/shard_map/ppermute | solution.py:689
  69.8 1.8 %collective-permute-done.20.refs_3_ = bf16[80,896]{1,0:T(8,128)(2,1)S(1)} collective-permute-done((bf16[80,896]{1,0:T(8,128)(2,1)S(1)}, bf16[80,896]{1,0:T(8,128)(2,1)S(1)}, u32[]{:S(2)}, u32[]{:S(2)}) %collective-permute-start.20) | collective-permute-done | bytes 143392 | tf_op jit(solution)/shard_map/ppermute | solution.py:689
  71.6 0.7 add.24
  (17 shorter events, 0.0 us)
Async XLA Ops:
  0.6 22.7 %collective-permute-start = (bf16[448,896]{1,0:T(8,128)(2,1)}, bf16[448,896]{1,0:T(8,128)(2,1)}, u32[]{:S(2)}, u32[]{:S(2)}) collective-permute-start(bf16[448,896]{1,0:T(8,128)(2,1)} %own_ref.7), channel_id=1, source_target_pairs={{0,4},{4,0},{8,12},{12,8},{16,20},{20,16},{24,28},{28,24},{1,5},{5... | collective-permute-start | bytes 2408456 | tf_op jit(solution)/shard_map/ppermute | solution.py:593
  1.2 43.3 %collective-permute-start.11 = (bf16[448,896]{1,0:T(8,128)(2,1)}, bf16[448,896]{1,0:T(8,128)(2,1)}, u32[]{:S(2)}, u32[]{:S(2)}) collective-permute-start(bf16[448,896]{1,0:T(8,128)(2,1)} %bitcast.20), channel_id=1, source_target_pairs={{0,4},{4,0},{8,12},{12,8},{16,20},{20,16},{24,28},{28,24},{1,5},{5... | collective-permute-start | bytes 2408456 | tf_op jit(solution)/shard_map/ppermute | solution.py:594
  3.5 11.4 %copy-start.11 = (bf16[80,896]{1,0:T(8,128)(2,1)S(1)}, bf16[80,896]{1,0:T(8,128)(2,1)}, u32[]{:S(2)}) copy-start(bf16[80,896]{1,0:T(8,128)(2,1)} %get-tuple-element.11.rest_1_) | copy-start | bytes 430084
  3.5 14.7 %copy-start.10 = (bf16[80,896]{1,0:T(8,128)(2,1)S(1)}, bf16[80,896]{1,0:T(8,128)(2,1)}, u32[]{:S(2)}) copy-start(bf16[80,896]{1,0:T(8,128)(2,1)} %get-tuple-element.12.rest_2_) | copy-start | bytes 430084
  3.5 16.5 %copy-start.9 = (bf16[80,896]{1,0:T(8,128)(2,1)S(1)}, bf16[80,896]{1,0:T(8,128)(2,1)}, u32[]{:S(2)}) copy-start(bf16[80,896]{1,0:T(8,128)(2,1)} %get-tuple-element.13.rest_3_) | copy-start | bytes 430084
  7.4 15.9 %copy-start = (bf16[448,896]{1,0:T(8,128)(2,1)S(1)}, bf16[448,896]{1,0:T(8,128)(2,1)}, u32[]{:S(2)}) copy-start(bf16[448,896]{1,0:T(8,128)(2,1)} %own_ref.7) | copy-start | bytes 2408452
  7.5 7.5 %collective-permute-start.9 = (bf16[384,128]{1,0:T(8,128)(2,1)}, bf16[384,128]{1,0:T(8,128)(2,1)S(1)}, u32[]{:S(2)}, u32[]{:S(2)}) collective-permute-start(bf16[384,128]{1,0:T(8,128)(2,1)} %get-tuple-element.17), channel_id=1, source_target_pairs={{0,24},{4,28},{8,16},{12,20},{16,8},{20,12},{24,0},{28,4},{1,25},{... | collective-permute-start | bytes 294920 | tf_op jit(solution)/shard_map/ppermute | solution.py:571
  11.4 5.6 %collective-permute-start.8 = (bf16[384,128]{1,0:T(8,128)(2,1)}, bf16[384,128]{1,0:T(8,128)(2,1)S(1)}, u32[]{:S(2)}, u32[]{:S(2)}) collective-permute-start(bf16[384,128]{1,0:T(8,128)(2,1)} %get-tuple-element.17), channel_id=1, source_target_pairs={{0,16},{4,20},{8,24},{12,28},{16,0},{20,4},{24,8},{28,12},{1,17},{... | collective-permute-start | bytes 294920 | tf_op jit(solution)/shard_map/ppermute | solution.py:571
  11.9 5.4 %collective-permute-start.7 = (bf16[384,128]{1,0:T(8,128)(2,1)}, bf16[384,128]{1,0:T(8,128)(2,1)S(1)}, u32[]{:S(2)}, u32[]{:S(2)}) collective-permute-start(bf16[384,128]{1,0:T(8,128)(2,1)} %get-tuple-element.17), channel_id=1, source_target_pairs={{0,8},{4,12},{8,0},{12,4},{16,24},{20,28},{24,16},{28,20},{1,9},{5... | collective-permute-start | bytes 294920 | tf_op jit(solution)/shard_map/ppermute | solution.py:571
  14.9 5.1 %collective-permute-start.1 = (bf16[80,896]{1,0:T(8,128)(2,1)S(1)}, bf16[80,896]{1,0:T(8,128)(2,1)S(1)}, u32[]{:S(2)}, u32[]{:S(2)}) collective-permute-start(bf16[80,896]{1,0:T(8,128)(2,1)S(1)} %copy-done.11), channel_id=1, source_target_pairs={{0,8},{4,12},{8,0},{12,4},{16,24},{20,28},{24,16},{28,20},{1,9},{5... | collective-permute-start | bytes 430088 | tf_op jit(solution)/shard_map/ppermute | solution.py:571
  18.2 17.3 %collective-permute-start.10 = (bf16[4,384,128]{2,1,0:T(8,128)(2,1)S(1)}, bf16[4,384,128]{2,1,0:T(8,128)(2,1)S(1)}, u32[]{:S(2)}, u32[]{:S(2)}) collective-permute-start(bf16[4,384,128]{2,1,0:T(8,128)(2,1)S(1)} %pad_maximum_fusion.1.rest_4_), channel_id=1, source_target_pairs={{0,4},{4,0},{8,12},{12,8},{16,20},{20,16},{24,28},{28,24},{1,5},{5... | collective-permute-start | bytes 1179656 | tf_op jit(solution)/shard_map/ppermute | solution.py:628
  18.3 8.8 %collective-permute-start.3 = (bf16[80,896]{1,0:T(8,128)(2,1)S(1)}, bf16[80,896]{1,0:T(8,128)(2,1)S(1)}, u32[]{:S(2)}, u32[]{:S(2)}) collective-permute-start(bf16[80,896]{1,0:T(8,128)(2,1)S(1)} %copy-done.10), channel_id=1, source_target_pairs={{0,16},{4,20},{8,24},{12,28},{16,0},{20,4},{24,8},{28,12},{1,17},{... | collective-permute-start | bytes 430088 | tf_op jit(solution)/shard_map/ppermute | solution.py:571
  20.1 10.5 %collective-permute-start.5 = (bf16[80,896]{1,0:T(8,128)(2,1)S(1)}, bf16[80,896]{1,0:T(8,128)(2,1)S(1)}, u32[]{:S(2)}, u32[]{:S(2)}) collective-permute-start(bf16[80,896]{1,0:T(8,128)(2,1)S(1)} %copy-done.9), channel_id=1, source_target_pairs={{0,24},{4,28},{8,16},{12,20},{16,8},{20,12},{24,0},{28,4},{1,25},{... | collective-permute-start | bytes 430088 | tf_op jit(solution)/shard_map/ppermute | solution.py:571
  24.9 10.7 %collective-permute-start.2 = (bf16[80,896]{1,0:T(8,128)(2,1)S(1)}, bf16[80,896]{1,0:T(8,128)(2,1)S(1)}, u32[]{:S(2)}, u32[]{:S(2)}) collective-permute-start(bf16[80,896]{1,0:T(8,128)(2,1)S(1)} %query_dot.5), channel_id=1, source_target_pairs={{0,8},{4,12},{8,0},{12,4},{16,24},{20,28},{24,16},{28,20},{1,9},{5... | collective-permute-start | bytes 430088 | tf_op jit(solution)/shard_map/ppermute | solution.py:571
  28.7 5.3 %copy-start.2 = (bf16[80,896]{1,0:T(8,128)(2,1)S(1)}, bf16[80,896]{1,0:T(8,128)(2,1)}, u32[]{:S(2)}) copy-start(bf16[80,896]{1,0:T(8,128)(2,1)} %get-tuple-element.10.rest_0_.rows_ref) | copy-start | bytes 430084
  28.7 7.6 %collective-permute-start.4 = (bf16[80,896]{1,0:T(8,128)(2,1)S(1)}, bf16[80,896]{1,0:T(8,128)(2,1)S(1)}, u32[]{:S(2)}, u32[]{:S(2)}) collective-permute-start(bf16[80,896]{1,0:T(8,128)(2,1)S(1)} %query_dot.6), channel_id=1, source_target_pairs={{0,16},{4,20},{8,24},{12,28},{16,0},{20,4},{24,8},{28,12},{1,17},{... | collective-permute-start | bytes 430088 | tf_op jit(solution)/shard_map/ppermute | solution.py:571
  32.1 6.1 %copy-start.3 = (f32[80,128]{1,0:T(8,128)S(1)}, f32[80,128]{1,0:T(8,128)}, u32[]{:S(2)}) copy-start(f32[80,128]{1,0:T(8,128)} %get-tuple-element.14.cosine_ref) | copy-start | bytes 122884
  32.1 6.1 %copy-start.4 = (f32[80,128]{1,0:T(8,128)S(1)}, f32[80,128]{1,0:T(8,128)}, u32[]{:S(2)}) copy-start(f32[80,128]{1,0:T(8,128)} %get-tuple-element.15.sine_ref) | copy-start | bytes 122884
  32.1 6.1 %collective-permute-start.6 = (bf16[80,896]{1,0:T(8,128)(2,1)S(1)}, bf16[80,896]{1,0:T(8,128)(2,1)S(1)}, u32[]{:S(2)}, u32[]{:S(2)}) collective-permute-start(bf16[80,896]{1,0:T(8,128)(2,1)S(1)} %query_dot.7), channel_id=1, source_target_pairs={{0,24},{4,28},{8,16},{12,20},{16,8},{20,12},{24,0},{28,4},{1,25},{... | collective-permute-start | bytes 430088 | tf_op jit(solution)/shard_map/ppermute | solution.py:571
  33.9 4.3 %copy-start.5 = (bf16[2,16,128]{2,1,0:T(8,128)(2,1)S(1)}, bf16[2,16,128]{2,1,0:T(8,128)(2,1)}, u32[]{:S(2)}) copy-start(bf16[2,16,128]{2,1,0:T(8,128)(2,1)} %get-tuple-element.16.own_ref) | copy-start | bytes 24580
  35.5 2.7 %copy-start.6 = (f32[896]{0:T(1024)S(1)}, f32[896]{0:T(1024)}, u32[]{:S(2)}) copy-start(f32[896]{0:T(1024)} %bias_ref.1) | copy-start | bytes 10756
  38.2 0.7 copy-start.7
  38.2 0.7 copy-start.8
  38.9 8.2 %copy-start.1 = (bf16[896,448]{0,1:T(8,128)(2,1)S(1)}, bf16[896,448]{0,1:T(8,128)(2,1)}, u32[]{:S(2)}) copy-start(bf16[896,448]{0,1:T(8,128)(2,1)} %param.25) | copy-start | bytes 2408452
  41.0 6.1 %collective-permute-start.16 = (bf16[80,896]{1,0:T(8,128)(2,1)S(1)}, bf16[80,896]{1,0:T(8,128)(2,1)S(1)}, u32[]{:S(2)}, u32[]{:S(2)}) collective-permute-start(bf16[80,896]{1,0:T(8,128)(2,1)S(1)} %attend.1.rows_ref), channel_id=1, source_target_pairs={{0,24},{4,28},{8,16},{12,20},{16,8},{20,12},{24,0},{28,4},{1,25},{... | collective-permute-start | bytes 430088 | tf_op jit(solution)/shard_map/ppermute | solution.py:571
  42.8 8.0 %collective-permute-start.14 = (bf16[80,896]{1,0:T(8,128)(2,1)S(1)}, bf16[80,896]{1,0:T(8,128)(2,1)S(1)}, u32[]{:S(2)}, u32[]{:S(2)}) collective-permute-start(bf16[80,896]{1,0:T(8,128)(2,1)S(1)} %attend.1.rows_ref), channel_id=1, source_target_pairs={{0,16},{4,20},{8,24},{12,28},{16,0},{20,4},{24,8},{28,12},{1,17},{... | collective-permute-start | bytes 430088 | tf_op jit(solution)/shard_map/ppermute | solution.py:571
  43.3 9.9 %collective-permute-start.12 = (bf16[80,896]{1,0:T(8,128)(2,1)S(1)}, bf16[80,896]{1,0:T(8,128)(2,1)S(1)}, u32[]{:S(2)}, u32[]{:S(2)}) collective-permute-start(bf16[80,896]{1,0:T(8,128)(2,1)S(1)} %attend.1.rows_ref), channel_id=1, source_target_pairs={{0,8},{4,12},{8,0},{12,4},{16,24},{20,28},{24,16},{28,20},{1,9},{5... | collective-permute-start | bytes 430088 | tf_op jit(solution)/shard_map/ppermute | solution.py:571
  48.9 9.2 %collective-permute-start.17 = (bf16[80,896]{1,0:T(8,128)(2,1)S(1)}, bf16[80,896]{1,0:T(8,128)(2,1)S(1)}, u32[]{:S(2)}, u32[]{:S(2)}) collective-permute-start(bf16[80,896]{1,0:T(8,128)(2,1)S(1)} %out_dot.7), channel_id=1, source_target_pairs={{0,24},{4,28},{8,16},{12,20},{16,8},{20,12},{24,0},{28,4},{1,25},{... | collective-permute-start | bytes 430088 | tf_op jit(solution)/shard_map/ppermute | solution.py:571
  52.6 5.5 %collective-permute-start.15 = (bf16[80,896]{1,0:T(8,128)(2,1)S(1)}, bf16[80,896]{1,0:T(8,128)(2,1)S(1)}, u32[]{:S(2)}, u32[]{:S(2)}) collective-permute-start(bf16[80,896]{1,0:T(8,128)(2,1)S(1)} %out_dot.6), channel_id=1, source_target_pairs={{0,16},{4,20},{8,24},{12,28},{16,0},{20,4},{24,8},{28,12},{1,17},{... | collective-permute-start | bytes 430088 | tf_op jit(solution)/shard_map/ppermute | solution.py:571
  55.1 5.2 %collective-permute-start.13 = (bf16[80,896]{1,0:T(8,128)(2,1)S(1)}, bf16[80,896]{1,0:T(8,128)(2,1)S(1)}, u32[]{:S(2)}, u32[]{:S(2)}) collective-permute-start(bf16[80,896]{1,0:T(8,128)(2,1)S(1)} %out_dot.5), channel_id=1, source_target_pairs={{0,8},{4,12},{8,0},{12,4},{16,24},{20,28},{24,16},{28,20},{1,9},{5... | collective-permute-start | bytes 430088 | tf_op jit(solution)/shard_map/ppermute | solution.py:571
  60.4 7.5 %collective-permute-start.18 = (bf16[80,896]{1,0:T(8,128)(2,1)S(1)}, bf16[80,896]{1,0:T(8,128)(2,1)S(1)}, u32[]{:S(2)}, u32[]{:S(2)}) collective-permute-start(bf16[80,896]{1,0:T(8,128)(2,1)S(1)} %get-tuple-element.20), channel_id=1, source_target_pairs={{0,1},{1,0},{2,3},{3,2},{4,5},{5,4},{6,7},{7,6},{8,9},{9,8},{10,11... | collective-permute-start | bytes 430088 | tf_op jit(solution)/shard_map/ppermute | solution.py:689
  62.0 7.8 %collective-permute-start.19 = (bf16[80,896]{1,0:T(8,128)(2,1)S(1)}, bf16[80,896]{1,0:T(8,128)(2,1)S(1)}, u32[]{:S(2)}, u32[]{:S(2)}) collective-permute-start(bf16[80,896]{1,0:T(8,128)(2,1)S(1)} %get-tuple-element.19), channel_id=1, source_target_pairs={{0,2},{1,3},{2,0},{3,1},{4,6},{5,7},{6,4},{7,5},{8,10},{9,11},{10,... | collective-permute-start | bytes 430088 | tf_op jit(solution)/shard_map/ppermute | solution.py:689
  64.6 7.0 %collective-permute-start.20 = (bf16[80,896]{1,0:T(8,128)(2,1)S(1)}, bf16[80,896]{1,0:T(8,128)(2,1)S(1)}, u32[]{:S(2)}, u32[]{:S(2)}) collective-permute-start(bf16[80,896]{1,0:T(8,128)(2,1)S(1)} %get-tuple-element.18), channel_id=1, source_target_pairs={{0,3},{1,2},{2,1},{3,0},{4,7},{5,6},{6,5},{7,4},{8,11},{9,10},{10,... | collective-permute-start | bytes 430088 | tf_op jit(solution)/shard_map/ppermute | solution.py:689
where the time goes:
time: 72.9 us; the launch traced here: 72.3 us
  starting transfers between devices  27.8 us (38%)
  Pallas kernels  22.5 us (31%)
  waiting for transfers between devices  19.3 us (26%)
  other arithmetic  1.03 us (1%)
  between operations  0.88 us (1%)
  local copies, waits for them, and re-layouts  0.76 us (1%)
    ppermute x15, starting transfers between devices, to_chip(): lax.ppermute(block, 'ctx', [(place, place ^ 2 * slot) for place in range(...  22.6 us
    ppermute x15, waiting for transfers between devices, to_chip(): lax.ppermute(block, 'ctx', [(place, place ^ 2 * slot) for place in range(...  12.5 us
    pallas_call x4, Pallas kernels, local_moving_rows(): pl.pallas_call(out_kernel, out_shape=bf16((row_count, columns)), in_specs...  7.35 us
    ppermute x3, waiting for transfers between devices, local_moving_rows(): lax.ppermute(columns_of(slot), 'tp', [(place, place ^ slot) for place in...  6.77 us
    pallas_call x4, Pallas kernels, local_moving_rows(): pl.pallas_call(query_kernel, out_shape=jax.ShapeDtypeStruct((row_count, c...  6.26 us
    ppermute x3, starting transfers between devices, local_moving_rows(): lax.ppermute(columns_of(slot), 'tp', [(place, place ^ slot) for place in...  4.45 us
    pallas_call x1, Pallas kernels, local_moving_rows(): pl.pallas_call(functools.partial(key_value_kernel, steps), out_shape=[bf1...  3.88 us
    pallas_call x1, Pallas kernels, local_moving_rows(): pl.pallas_call(norm_kernel, out_shape=[bf16((row_count, chip_width))] * c...  2.24 us
  transfers between devices with their start and end apart: 21, of which 11 were waited for; matrix products, arithmetic and copies ran while one was open for 1% of the time, Pallas kernels for 30%

commit v1 on v0

--- a/solution.py
+++ b/solution.py
@@ -289,11 +289,11 @@
     sample_prompt_ref,
     *rest,
 ):
-    chips = len(rest) - 16
-    message_refs, rest = rest[:chips], rest[chips:]
+    chips = (len(rest) - 16) // 2
+    message_hbm, rest = rest[:chips], rest[chips:]
     (key_weight_hbm, value_weight_hbm, *other_hbm), rest = rest[:6], rest[6:]
     (packed_ref, own_ref, cosine_ref, sine_ref), rest = rest[:4], rest[4:]
-    weight_ref, *fetched, semaphores = rest
+    message_refs, (weight_ref, *fetched, semaphores) = rest[:chips], rest[chips:]
     key_bias_ref, value_bias_ref, cache_keys_ref, cache_values_ref = fetched[:4]
     prompts, prefix_dev, width = cache_keys_ref.shape
     copies = [
@@ -304,6 +304,7 @@
                 (value_weight_hbm, weight_ref.at[:, width:]),
             ]
             + list(zip(other_hbm, fetched))
+            + list(zip(message_hbm, message_refs))
         )
     ]
     for copy in copies:
@@ -374,33 +375,68 @@
         product(other_ref, own_ref)
 
 
-def out_kernel(core_ref, rows_ref, own_ref, other_ref, out_ref):
+def turn_kernel(core_ref, own_ref, other_ref, out_ref):
     half = own_ref.shape[0]
-    rows = rows_ref[...]
-
-    def product(weight_ref):
-        return lax.dot_general(
-            rows, weight_ref[...], (((1,), (1,)), ((), ())), preferred_element_type=jnp.float32
-        ).astype(out_ref.dtype)
 
     @pl.when(core_ref[0] == 0)
     def _():
-        out_ref[:, :half] = product(own_ref)
-        out_ref[:, half:] = product(other_ref)
+        out_ref[:, :half] = own_ref[...].T
+        out_ref[:, half:] = other_ref[...].T
 
     @pl.when(core_ref[0] == 1)
     def _():
-        out_ref[:, :half] = product(other_ref)
-        out_ref[:, half:] = product(own_ref)
+        out_ref[:, :half] = other_ref[...].T
+        out_ref[:, half:] = own_ref[...].T
+
+
+def out_kernel(rows_ref, weight_ref, out_ref):
+    out_ref[...] = jnp.dot(
+        rows_ref[...], weight_ref[...], preferred_element_type=jnp.float32
+    ).astype(out_ref.dtype)
+
+
+def own_query_kernel(
+    prefix_dev,
+    group,
+    core_ref,
+    ctx_ref,
+    lengths_ref,
+    sample_prompt_ref,
+    rows_ref,
+    own_ref,
+    other_ref,
+    bias_ref,
+    *rest,
+):
+    staged_refs, share_ref, rest = rest[:3], rest[3], rest[4:]
+    staged_outs, span_limit_ref, step_limit_ref = rest[:3], rest[3], rest[4]
+    query_kernel(core_ref, rows_ref, own_ref, other_ref, share_ref)
+    share_ref[...] += bias_ref[...][None, :]
+    for staged_ref, staged_out in zip(staged_refs, staged_outs):
+        staged_out[...] = staged_ref[...]
+    prompts, span_rows, _ = span_limit_ref.shape
+    own_rows = staged_refs[2].shape[1]
+    samples = sample_prompt_ref.shape[0]
+    span_dev = span_rows // group
+    row_index = lax.broadcasted_iota(jnp.int32, (span_rows, 1), 0)
+    query_places = ctx_ref[1] * prefix_dev + ctx_ref[0] * span_dev + lax.rem(row_index, span_dev)
+    row_index = lax.broadcasted_iota(jnp.int32, (group * own_rows, 1), 0)
+    sample = lax.rem(row_index, samples)
+    for prompt in range(prompts):
+        span_limit_ref[prompt] = jnp.minimum(query_places, lengths_ref[prompt] - 1)
+        limit = jnp.full(row_index.shape, -1, jnp.int32)
+        for index in range(samples):
+            reach = jnp.where(sample_prompt_ref[index] == prompt, lengths_ref[prompt] - 1, -1)
+            limit = jnp.where(sample == index, reach, limit)
+        step_limit_ref[prompt] = limit
 
 
 def attend_kernel(
     steps,
     prefix_dev,
     ctx_ref,
-    lengths_ref,
-    sample_prompt_ref,
-    bias_ref,
+    span_limit_ref,
+    step_limit_ref,
     cosine_ref,
     sine_ref,
     own_ref,
@@ -408,12 +444,11 @@
 ):
     *query_refs, near_ref, far_ref, out_ref, rotated = rest
     packed_refs = (near_ref, far_ref)
-    prompts = lengths_ref.shape[0]
-    samples = sample_prompt_ref.shape[0]
-    own_rows = steps * samples
+    prompts = span_limit_ref.shape[0]
+    own_rows, kv_width = own_ref.shape[1:]
+    samples = own_rows // steps
     row_count, columns = out_ref.shape
     span_dev = (row_count - own_rows) // prompts
-    kv_width = own_ref.shape[2]
     kv_local = kv_width // HEAD
     heads_local = columns // HEAD
     group = heads_local // kv_local
@@ -424,7 +459,6 @@
         total = query_refs[0][:, span].astype(jnp.float32)
         for query_ref in query_refs[1:]:
             total = total + query_ref[:, span].astype(jnp.float32)
-        total = total + bias_ref[span][None, :]
         rotated[:, span] = rotate_block(total, cosine, sine).astype(jnp.bfloat16)
     chips, packed_rows, _ = near_ref.shape
     block = packed_rows // (2 * prompts)
@@ -476,12 +510,9 @@
         first_head = group_index * group
         keys = [cached(0, prompt, group_index) for prompt in range(prompts)]
         values = [cached(1, prompt, group_index) for prompt in range(prompts)]
-        row_index = lax.broadcasted_iota(jnp.int32, (group * span_dev, 1), 0)
-        query_places = prefix_all + ctx_ref[0] * span_dev + lax.rem(row_index, span_dev)
         for prompt in range(prompts):
             queries = rows_of(prompt * span_dev, span_dev, first_head)
-            limit = jnp.minimum(query_places, lengths_ref[prompt] - 1)
-            scores = score(queries, keys[prompt], places <= limit)
+            scores = score(queries, keys[prompt], places <= span_limit_ref[prompt])
             highest = jnp.max(scores, axis=-1, keepdims=True)
             weights = jnp.exp2(scores - highest)
             totals = jnp.sum(weights, axis=-1, keepdims=True)
@@ -503,13 +534,7 @@
         own_lanes = slice(group_index * HEAD, (group_index + 1) * HEAD)
         parts = [score(queries, own_ref[0, :, own_lanes], own_visible)]
         for prompt in range(prompts):
-            limit = jnp.full(row_index.shape, -1, jnp.int32)
-            for index in range(samples):
-                reach = jnp.where(
-                    sample_prompt_ref[index] == prompt, lengths_ref[prompt] - 1, -1
-                )
-                limit = jnp.where(sample == index, reach, limit)
-            parts.append(score(queries, keys[prompt], places <= limit))
+            parts.append(score(queries, keys[prompt], places <= step_limit_ref[prompt]))
         highest = functools.reduce(
             jnp.maximum, [jnp.max(part, axis=-1, keepdims=True) for part in parts]
         )
@@ -602,14 +627,15 @@
             table,
             table,
         ],
-        in_specs=[SMEM] * 3 + [VMEM] * chips + [HBM] * 6,
+        in_specs=[SMEM] * 3 + [HBM] * (chips + 6),
         out_specs=[VMEM] * 4,
-        scratch_shapes=[pltpu.VMEM((model, 2 * kv_width), jnp.bfloat16)]
+        scratch_shapes=[pltpu.VMEM((row_count, chip_width), jnp.bfloat16)] * chips
+        + [pltpu.VMEM((model, 2 * kv_width), jnp.bfloat16)]
         + [
             pltpu.VMEM(array.shape, array.dtype)
             for array in (key_bias, value_bias, cache_keys, cache_values)
         ]
-        + [pltpu.SemaphoreType.DMA((6,))],
+        + [pltpu.SemaphoreType.DMA((chips + 6,))],
         compiler_params=KEY_VALUE_KERNEL,
         name="key_value",
     )(
@@ -627,35 +653,62 @@
     near_packed = jnp.stack([packed] + [to_chip(packed, slot) for slot in range(1, chips)])
     far_packed = lax.ppermute(near_packed, "ctx", core_pairs)
 
-    shares = []
+    shares, later = [], []
+    group = columns // kv_width
     for slot, rows in enumerate(inbound):
-        partial = pl.pallas_call(
-            query_kernel,
-            out_shape=jax.ShapeDtypeStruct(
-                (row_count, columns), jnp.bfloat16 if slot else jnp.float32
-            ),
-            in_specs=[SMEM] + [VMEM] * 3,
-            out_specs=VMEM,
-            compiler_params=KERNEL,
-            name="query_dot",
-        )(core_place.reshape(1), rows, query_weight, other_query)
+        weights = (core_place.reshape(1), rows, query_weight, other_query)
+        if slot:
+            partial = pl.pallas_call(
+                query_kernel,
+                out_shape=bf16((row_count, columns)),
+                in_specs=[SMEM] + [VMEM] * 3,
+                out_specs=VMEM,
+                compiler_params=KERNEL,
+                name="query_dot",
+            )(*weights)
+        else:
+            partial, *later = pl.pallas_call(
+                functools.partial(own_query_kernel, prefix_dev, group),
+                out_shape=[
+                    jax.ShapeDtypeStruct((row_count, columns), jnp.float32),
+                    table,
+                    table,
+                    bf16(own.shape),
+                    jax.ShapeDtypeStruct((prompts, group * span_dev, 1), jnp.int32),
+                    jax.ShapeDtypeStruct((prompts, group * steps * samples, 1), jnp.int32),
+                ],
+                in_specs=[SMEM] * 4 + [VMEM] * 7,
+                out_specs=[VMEM] * 6,
+                compiler_params=KERNEL,
+                name="query_own",
+            )(
+                core_place.reshape(1),
+                jnp.stack([ctx_place, jnp.int32(ctx_size)]),
+                lengths,
+                sample_prompt,
+                *weights[1:],
+                query_bias,
+                cosine,
+                sine,
+                own,
+            )
         if slot:
             partial = to_chip(partial, slot)
         shares.append(partial)
+    cosine, sine, own, span_limit, step_limit = later
 
     attention = pl.pallas_call(
         functools.partial(attend_kernel, steps, prefix_dev),
         out_shape=bf16((row_count, columns)),
-        in_specs=[SMEM] * 3 + [VMEM] * (4 + chips + 2),
+        in_specs=[SMEM] + [VMEM] * (5 + chips + 2),
         out_specs=VMEM,
         scratch_shapes=[pltpu.VMEM((row_count, columns), jnp.bfloat16)],
         compiler_params=KERNEL,
         name="attend",
     )(
         ctx_place.reshape(1),
-        lengths,
-        sample_prompt,
-        query_bias,
+        span_limit,
+        step_limit,
         cosine,
         sine,
         own,
@@ -664,17 +717,25 @@
         far_packed,
     )
 
+    chip_out = pl.pallas_call(
+        turn_kernel,
+        out_shape=bf16((columns, 2 * out_weight.shape[1])),
+        in_specs=[SMEM] + [VMEM] * 2,
+        out_specs=VMEM,
+        compiler_params=KERNEL,
+        name="out_turn",
+    )(core_place.reshape(1), out_weight.T, other_out)
     attended = [attention] + [to_chip(attention, slot) for slot in range(1, chips)]
     returned = []
     for slot, rows in enumerate(attended):
         terms = pl.pallas_call(
             out_kernel,
             out_shape=bf16((row_count, columns)),
-            in_specs=[SMEM] + [VMEM] * 3,
+            in_specs=[VMEM] * 2,
             out_specs=VMEM,
             compiler_params=KERNEL,
             name="out_dot",
-        )(core_place.reshape(1), rows, out_weight.T, other_out)
+        )(rows, chip_out)
         if slot:
             terms = to_chip(terms, slot)
         returned.append(terms)

time: 72.9 us -> 68.6 us (0.941)
  Pallas kernels: 22.5 us -> 18.1 us
    pallas_call x4, Pallas kernels: 7.35 us -> 1.47 us  [local_moving_rows(): pl.pallas_call(out_kernel, out_shape=bf16((row_count, columns)), in_specs...]
    pallas_call x4 -> x5, Pallas kernels: 6.26 us -> 8.35 us  [the longest x3 4.69 us: local_moving_rows(): pl.pallas_call(query_kernel, out_shape=bf16((row_count, columns)), in_spe...]
  transfers between devices with their start and end apart: 21 -> 21, of which waited for: 11 -> 13; matrix products, arithmetic and copies ran while one was open for 1% -> 1% of each run, Pallas kernels for 30% -> 25%
where the time goes in v1:
time: 68.6 us; the launch traced here: 68.2 us
  starting transfers between devices  28.2 us (41%)
  waiting for transfers between devices  19.7 us (29%)
  Pallas kernels  18.1 us (26%)
  other arithmetic  1.11 us (2%)
  between operations  0.92 us (1%)
    ppermute x15, starting transfers between devices, to_chip(): lax.ppermute(block, 'ctx', [(place, place ^ 2 * slot) for place in range(...  23.1 us
    ppermute x15, waiting for transfers between devices, to_chip(): lax.ppermute(block, 'ctx', [(place, place ^ 2 * slot) for place in range(...  13.1 us
    ppermute x3, waiting for transfers between devices, local_moving_rows(): lax.ppermute(columns_of(slot), 'tp', [(place, place ^ slot) for place in...  6.66 us
    pallas_call x3, Pallas kernels, local_moving_rows(): pl.pallas_call(query_kernel, out_shape=bf16((row_count, columns)), in_spe...  4.69 us
    ppermute x3, starting transfers between devices, local_moving_rows(): lax.ppermute(columns_of(slot), 'tp', [(place, place ^ slot) for place in...  4.45 us
    pallas_call x1, Pallas kernels, local_moving_rows(): pl.pallas_call(functools.partial(key_value_kernel, steps), out_shape=[bf1...  3.72 us
    pallas_call x1, Pallas kernels, local_moving_rows(): pl.pallas_call(norm_kernel, out_shape=[bf16((row_count, chip_width))] * c...  2.25 us
    pallas_call x1, Pallas kernels, local_moving_rows(): pl.pallas_call(turn_kernel, out_shape=bf16((columns, 2 * out_weight.shape...  1.92 us
  transfers between devices with their start and end apart: 21, of which 13 were waited for; matrix products, arithmetic and copies ran while one was open for 1% of the time, Pallas kernels for 25%

profile of v1, /device:TPU:0, one launch (start us, length us, event | category | flops | bytes accessed | tf_op | source)
XLA Modules:
  0.0 68.2 jit_solution(618485104596701013)
XLA Ops:
  0.6 0.6 collective-permute-start
  1.2 0.1 collective-permute-start.11
  1.3 2.3 %norm.1 = (bf16[80,896]{1,0:T(8,128)(2,1)}, bf16[80,896]{1,0:T(8,128)(2,1)}, bf16[80,896]{1,0:T(8,128)(2,1)}, bf16[80,896]{1,0:T(8,128)(2,1)}) custom-call(s32[1]{0:T(128)} %bitcast.2.place_ref, bf16[2,32,3584]{2,1,0:T(8,128)(2,1)} %span_hbm.1, bf16[4,4,3584]{2,1,0:T(4,128)(2,1)} %step_hbm.1, f32[3584]{0:T(1024)} %gain_hbm.1), custom_call_target="tpu_custom_call" | custom-call | tf_op jit(solution)/shard_map/norm/pallas_call | solution.py:601
  3.6 0.0 copy-start
  3.6 3.7 %key_value.1 = (bf16[384,128]{1,0:T(8,128)(2,1)}, bf16[2,16,128]{2,1,0:T(8,128)(2,1)}, f32[80,128]{1,0:T(8,128)}, f32[80,128]{1,0:T(8,128)}) custom-call(s32[1]{0:T(128)} %bitcast.ctx_ref, s32[2]{0:T(128)} %lengths_ref.3, s32[4]{0:T(128)} %sample_prompt_ref.3, bf16[80,896]{1,0:T(8,128)(2,1)} %get-tuple-element.16.rest_0_.rows_ref, ...), custom_call_target="tpu_custom_call" | custom-call | tf_op jit(solution)/shard_map/key_value/pallas_call | solution.py:622
  7.3 3.9 %collective-permute-start.9 = (bf16[384,128]{1,0:T(8,128)(2,1)}, bf16[384,128]{1,0:T(8,128)(2,1)S(1)}, u32[]{:S(2)}, u32[]{:S(2)}) collective-permute-start(bf16[384,128]{1,0:T(8,128)(2,1)} %get-tuple-element.29), channel_id=1, source_target_pairs={{0,24},{4,28},{8,16},{12,20},{16,8},{20,12},{24,0},{28,4},{1,25},{... | collective-permute-start | bytes 294920 | tf_op jit(solution)/shard_map/ppermute | solution.py:596
  11.2 0.5 collective-permute-start.8
  11.7 0.1 collective-permute-start.7
  11.9 2.9 %collective-permute-done.9 = bf16[384,128]{1,0:T(8,128)(2,1)S(1)} collective-permute-done((bf16[384,128]{1,0:T(8,128)(2,1)}, bf16[384,128]{1,0:T(8,128)(2,1)S(1)}, u32[]{:S(2)}, u32[]{:S(2)}) %collective-permute-start.9) | collective-permute-done | bytes 98336 | tf_op jit(solution)/shard_map/ppermute | solution.py:596
  14.8 2.0 %collective-permute-start.1 = (bf16[80,896]{1,0:T(8,128)(2,1)S(1)}, bf16[80,896]{1,0:T(8,128)(2,1)S(1)}, u32[]{:S(2)}, u32[]{:S(2)}) collective-permute-start(bf16[80,896]{1,0:T(8,128)(2,1)S(1)} %copy-done.11), channel_id=1, source_target_pairs={{0,8},{4,12},{8,0},{12,4},{16,24},{20,28},{24,16},{28,20},{1,9},{5... | collective-permute-start | bytes 430088 | tf_op jit(solution)/shard_map/ppermute | solution.py:596
  16.8 0.0 collective-permute-done.8
  16.8 0.3 collective-permute-done.7
  17.1 0.9 %pad_maximum_fusion.1.rest_4_ = bf16[4,384,128]{2,1,0:T(8,128)(2,1)S(1)} fusion(bf16[1,384,128]{2,1,0:T(8,128)(2,1)S(1)} %bitcast.27, bf16[1,384,128]{2,1,0:T(8,128)(2,1)S(1)} %bitcast.28, bf16[1,384,128]{2,1,0:T(8,128)(2,1)S(1)} %bitcast.29, bf16[1,384,128]{2,1,0:T(8,128)(2,1)} %bitcast.26), kind=kLoop, calls=%fused_computation.1 | loop fusion | flops 589824 | bytes 786432 | tf_op jit(solution)/shard_map/stack | solution.py:653
  18.0 0.1 collective-permute-start.10
  18.1 1.6 %collective-permute-start.3 = (bf16[80,896]{1,0:T(8,128)(2,1)S(1)}, bf16[80,896]{1,0:T(8,128)(2,1)S(1)}, u32[]{:S(2)}, u32[]{:S(2)}) collective-permute-start(bf16[80,896]{1,0:T(8,128)(2,1)S(1)} %copy-done.10), channel_id=1, source_target_pairs={{0,16},{4,20},{8,24},{12,28},{16,0},{20,4},{24,8},{28,12},{1,17},{... | collective-permute-start | bytes 430088 | tf_op jit(solution)/shard_map/ppermute | solution.py:596
  19.7 0.2 collective-permute-done.1.rows_ref
  19.9 3.2 %collective-permute-start.5 = (bf16[80,896]{1,0:T(8,128)(2,1)S(1)}, bf16[80,896]{1,0:T(8,128)(2,1)S(1)}, u32[]{:S(2)}, u32[]{:S(2)}) collective-permute-start(bf16[80,896]{1,0:T(8,128)(2,1)S(1)} %copy-done.9), channel_id=1, source_target_pairs={{0,24},{4,28},{8,16},{12,20},{16,8},{20,12},{24,0},{28,4},{1,25},{... | collective-permute-start | bytes 430088 | tf_op jit(solution)/shard_map/ppermute | solution.py:596
  23.2 0.0 collective-permute-done.other_ref
  23.2 1.6 %query_dot.3 = bf16[80,896]{1,0:T(8,128)(2,1)S(1)} custom-call(s32[1]{0:T(128)} %bitcast.1.core_ref, bf16[80,896]{1,0:T(8,128)(2,1)S(1)} %collective-permute-done.1.rows_ref, bf16[448,896]{1,0:T(8,128)(2,1)S(1)} %copy-done, bf16[448,896]{1,0:T(8,128)(2,1)} %collective-permute-done.other_ref), custom_call_target="tpu_custom_call" | custom-call | tf_op jit(solution)/shard_map/query_dot/pallas_call | solution.py:661
  24.8 0.0 copy-start.5
  24.8 0.0 copy-start.6
  24.8 0.0 copy-start.7
  24.8 0.0 copy-start.8
  24.8 0.3 collective-permute-start.2
  25.1 1.9 %collective-permute-done.3.rows_ref = bf16[80,896]{1,0:T(8,128)(2,1)S(1)} collective-permute-done((bf16[80,896]{1,0:T(8,128)(2,1)S(1)}, bf16[80,896]{1,0:T(8,128)(2,1)S(1)}, u32[]{:S(2)}, u32[]{:S(2)}) %collective-permute-start.3) | collective-permute-done | bytes 143392 | tf_op jit(solution)/shard_map/ppermute | solution.py:596
  27.0 1.6 %query_dot.4 = bf16[80,896]{1,0:T(8,128)(2,1)S(1)} custom-call(s32[1]{0:T(128)} %bitcast.1.core_ref, bf16[80,896]{1,0:T(8,128)(2,1)S(1)} %collective-permute-done.3.rows_ref, bf16[448,896]{1,0:T(8,128)(2,1)S(1)} %copy-done, bf16[448,896]{1,0:T(8,128)(2,1)} %collective-permute-done.other_ref), custom_call_target="tpu_custom_call" | custom-call | tf_op jit(solution)/shard_map/query_dot/pallas_call | solution.py:661
  28.6 1.9 %collective-permute-start.4 = (bf16[80,896]{1,0:T(8,128)(2,1)S(1)}, bf16[80,896]{1,0:T(8,128)(2,1)S(1)}, u32[]{:S(2)}, u32[]{:S(2)}) collective-permute-start(bf16[80,896]{1,0:T(8,128)(2,1)S(1)} %query_dot.4), channel_id=1, source_target_pairs={{0,16},{4,20},{8,24},{12,28},{16,0},{20,4},{24,8},{28,12},{1,17},{... | collective-permute-start | bytes 430088 | tf_op jit(solution)/shard_map/ppermute | solution.py:596
  30.5 0.0 collective-permute-done.5.rows_ref
  30.5 1.6 %query_dot.5 = bf16[80,896]{1,0:T(8,128)(2,1)S(1)} custom-call(s32[1]{0:T(128)} %bitcast.1.core_ref, bf16[80,896]{1,0:T(8,128)(2,1)S(1)} %collective-permute-done.5.rows_ref, bf16[448,896]{1,0:T(8,128)(2,1)S(1)} %copy-done, bf16[448,896]{1,0:T(8,128)(2,1)} %collective-permute-done.other_ref), custom_call_target="tpu_custom_call" | custom-call | tf_op jit(solution)/shard_map/query_dot/pallas_call | solution.py:661
  32.0 1.7 %collective-permute-start.6 = (bf16[80,896]{1,0:T(8,128)(2,1)S(1)}, bf16[80,896]{1,0:T(8,128)(2,1)S(1)}, u32[]{:S(2)}, u32[]{:S(2)}) collective-permute-start(bf16[80,896]{1,0:T(8,128)(2,1)S(1)} %query_dot.5), channel_id=1, source_target_pairs={{0,24},{4,28},{8,16},{12,20},{16,8},{20,12},{24,0},{28,4},{1,25},{... | collective-permute-start | bytes 430088 | tf_op jit(solution)/shard_map/ppermute | solution.py:596
  33.8 0.1 pad_add_fusion.ctx_ref
  33.9 0.0 copy-start.1
  33.9 1.7 %query_own.1 = (f32[80,896]{1,0:T(8,128)S(1)}, f32[80,128]{1,0:T(8,128)S(1)}, f32[80,128]{1,0:T(8,128)S(1)}, bf16[2,16,128]{2,1,0:T(8,128)(2,1)S(1)}, s32[2,224,...) custom-call(s32[1]{0:T(128)} %bitcast.1.core_ref, s32[2]{0:T(128)S(1)} %pad_add_fusion.ctx_ref, s32[2]{0:T(128)S(1)} %copy-done.7, ...), custom_call_target="tpu_custom_call" | custom-call | tf_op jit(solution)/shard_map/query_own/pallas_call | solution.py:670
  35.6 0.0 collective-permute-done.10.rest_5_
  35.6 0.0 collective-permute-done.2.rest_1_
  35.6 0.5 collective-permute-done.4.rest_2_
  36.2 1.9 %collective-permute-done.6.rest_3_ = bf16[80,896]{1,0:T(8,128)(2,1)S(1)} collective-permute-done((bf16[80,896]{1,0:T(8,128)(2,1)S(1)}, bf16[80,896]{1,0:T(8,128)(2,1)S(1)}, u32[]{:S(2)}, u32[]{:S(2)}) %collective-permute-start.6) | collective-permute-done | bytes 143392 | tf_op jit(solution)/shard_map/ppermute | solution.py:596
  38.1 1.6 %attend.1.rows_ref = bf16[80,896]{1,0:T(8,128)(2,1)S(1)} custom-call(s32[1]{0:T(128)} %bitcast.ctx_ref, s32[2,224,1]{2,1,0:T(8,128)S(1)} %get-tuple-element.23.span_limit_ref, s32[2,112,1]{2,1,0:T(8,128)S(1)} %get-tuple-element.24.step_limit_ref, f32[80,128]{1,0:T(8,128)S(1)} %get-tuple-element.25.cosine_ref, f32[80,128]{1,0:T(8,128)S(1)} %get-tuple-element.26.sine_ref, ...), custom_call_target="tpu_custom_call" | custom-call | tf_op jit(solution)/shard_map/attend/pallas_call | solution.py:700
  39.7 1.7 %collective-permute-start.16 = (bf16[80,896]{1,0:T(8,128)(2,1)S(1)}, bf16[80,896]{1,0:T(8,128)(2,1)S(1)}, u32[]{:S(2)}, u32[]{:S(2)}) collective-permute-start(bf16[80,896]{1,0:T(8,128)(2,1)S(1)} %attend.1.rows_ref), channel_id=1, source_target_pairs={{0,24},{4,28},{8,16},{12,20},{16,8},{20,12},{24,0},{28,4},{1,25},{... | collective-permute-start | bytes 430088 | tf_op jit(solution)/shard_map/ppermute | solution.py:596
  41.4 0.5 collective-permute-start.14
  41.9 1.3 %collective-permute-start.12 = (bf16[80,896]{1,0:T(8,128)(2,1)S(1)}, bf16[80,896]{1,0:T(8,128)(2,1)S(1)}, u32[]{:S(2)}, u32[]{:S(2)}) collective-permute-start(bf16[80,896]{1,0:T(8,128)(2,1)S(1)} %attend.1.rows_ref), channel_id=1, source_target_pairs={{0,8},{4,12},{8,0},{12,4},{16,24},{20,28},{24,16},{28,20},{1,9},{5... | collective-permute-start | bytes 430088 | tf_op jit(solution)/shard_map/ppermute | solution.py:596
  43.2 0.0 collective-permute-done.11.other_ref
  43.2 1.9 %out_turn.1.weight_ref = bf16[896,896]{1,0:T(8,128)(2,1)S(1)} custom-call(s32[1]{0:T(128)} %bitcast.1.core_ref, bf16[448,896]{1,0:T(8,128)(2,1)S(1)} %bitcast.21, bf16[448,896]{1,0:T(8,128)(2,1)} %collective-permute-done.11.other_ref), custom_call_target="tpu_custom_call" | custom-call | tf_op jit(solution)/shard_map/out_turn/pallas_call | solution.py:720
  45.2 0.7 collective-permute-done.16.rows_ref
  45.8 0.4 out_dot.7
  46.2 1.8 %collective-permute-start.17 = (bf16[80,896]{1,0:T(8,128)(2,1)S(1)}, bf16[80,896]{1,0:T(8,128)(2,1)S(1)}, u32[]{:S(2)}, u32[]{:S(2)}) collective-permute-start(bf16[80,896]{1,0:T(8,128)(2,1)S(1)} %out_dot.7), channel_id=1, source_target_pairs={{0,24},{4,28},{8,16},{12,20},{16,8},{20,12},{24,0},{28,4},{1,25},{... | collective-permute-start | bytes 430088 | tf_op jit(solution)/shard_map/ppermute | solution.py:596
  48.0 1.5 %collective-permute-done.14.rows_ref = bf16[80,896]{1,0:T(8,128)(2,1)S(1)} collective-permute-done((bf16[80,896]{1,0:T(8,128)(2,1)S(1)}, bf16[80,896]{1,0:T(8,128)(2,1)S(1)}, u32[]{:S(2)}, u32[]{:S(2)}) %collective-permute-start.14) | collective-permute-done | bytes 143392 | tf_op jit(solution)/shard_map/ppermute | solution.py:596
  49.5 0.4 out_dot.6
  49.9 0.8 %collective-permute-start.15 = (bf16[80,896]{1,0:T(8,128)(2,1)S(1)}, bf16[80,896]{1,0:T(8,128)(2,1)S(1)}, u32[]{:S(2)}, u32[]{:S(2)}) collective-permute-start(bf16[80,896]{1,0:T(8,128)(2,1)S(1)} %out_dot.6), channel_id=1, source_target_pairs={{0,16},{4,20},{8,24},{12,28},{16,0},{20,4},{24,8},{28,12},{1,17},{... | collective-permute-start | bytes 430088 | tf_op jit(solution)/shard_map/ppermute | solution.py:596
  50.7 0.4 out_dot.5
  51.0 1.6 %collective-permute-start.13 = (bf16[80,896]{1,0:T(8,128)(2,1)S(1)}, bf16[80,896]{1,0:T(8,128)(2,1)S(1)}, u32[]{:S(2)}, u32[]{:S(2)}) collective-permute-start(bf16[80,896]{1,0:T(8,128)(2,1)S(1)} %out_dot.5), channel_id=1, source_target_pairs={{0,8},{4,12},{8,0},{12,4},{16,24},{20,28},{24,16},{28,20},{1,9},{5... | collective-permute-start | bytes 430088 | tf_op jit(solution)/shard_map/ppermute | solution.py:596
  52.7 0.4 out_dot.4
  53.0 0.0 collective-permute-done.17
  53.0 2.0 %collective-permute-done.15 = bf16[80,896]{1,0:T(8,128)(2,1)S(1)} collective-permute-done((bf16[80,896]{1,0:T(8,128)(2,1)S(1)}, bf16[80,896]{1,0:T(8,128)(2,1)S(1)}, u32[]{:S(2)}, u32[]{:S(2)}) %collective-permute-start.15) | collective-permute-done | bytes 143392 | tf_op jit(solution)/shard_map/ppermute | solution.py:596
  55.0 1.2 %collective-permute-done.13 = bf16[80,896]{1,0:T(8,128)(2,1)S(1)} collective-permute-done((bf16[80,896]{1,0:T(8,128)(2,1)S(1)}, bf16[80,896]{1,0:T(8,128)(2,1)S(1)}, u32[]{:S(2)}, u32[]{:S(2)}) %collective-permute-start.13) | collective-permute-done | bytes 143392 | tf_op jit(solution)/shard_map/ppermute | solution.py:596
  56.2 0.1 pad_maximum_fusion
  56.3 0.1 dynamic-slice_bitcast_fusion
  56.4 1.6 %collective-permute-start.18 = (bf16[80,896]{1,0:T(8,128)(2,1)S(1)}, bf16[80,896]{1,0:T(8,128)(2,1)S(1)}, u32[]{:S(2)}, u32[]{:S(2)}) collective-permute-start(bf16[80,896]{1,0:T(8,128)(2,1)S(1)} %get-tuple-element.32), channel_id=1, source_target_pairs={{0,1},{1,0},{2,3},{3,2},{4,5},{5,4},{6,7},{7,6},{8,9},{9,8},{10,11... | collective-permute-start | bytes 430088 | tf_op jit(solution)/shard_map/ppermute | solution.py:750
  57.9 2.6 %collective-permute-start.19 = (bf16[80,896]{1,0:T(8,128)(2,1)S(1)}, bf16[80,896]{1,0:T(8,128)(2,1)S(1)}, u32[]{:S(2)}, u32[]{:S(2)}) collective-permute-start(bf16[80,896]{1,0:T(8,128)(2,1)S(1)} %get-tuple-element.31), channel_id=1, source_target_pairs={{0,2},{1,3},{2,0},{3,1},{4,6},{5,7},{6,4},{7,5},{8,10},{9,11},{10,... | collective-permute-start | bytes 430088 | tf_op jit(solution)/shard_map/ppermute | solution.py:750
  60.5 0.3 collective-permute-start.20
  60.8 0.7 %collective-permute-done.18.refs_1_ = bf16[80,896]{1,0:T(8,128)(2,1)S(1)} collective-permute-done((bf16[80,896]{1,0:T(8,128)(2,1)S(1)}, bf16[80,896]{1,0:T(8,128)(2,1)S(1)}, u32[]{:S(2)}, u32[]{:S(2)}) %collective-permute-start.18) | collective-permute-done | bytes 143392 | tf_op jit(solution)/shard_map/ppermute | solution.py:750
  61.5 3.9 %collective-permute-done.19.refs_2_ = bf16[80,896]{1,0:T(8,128)(2,1)S(1)} collective-permute-done((bf16[80,896]{1,0:T(8,128)(2,1)S(1)}, bf16[80,896]{1,0:T(8,128)(2,1)S(1)}, u32[]{:S(2)}, u32[]{:S(2)}) %collective-permute-start.19) | collective-permute-done | bytes 143392 | tf_op jit(solution)/shard_map/ppermute | solution.py:750
  65.5 2.0 %collective-permute-done.20.refs_3_ = bf16[80,896]{1,0:T(8,128)(2,1)S(1)} collective-permute-done((bf16[80,896]{1,0:T(8,128)(2,1)S(1)}, bf16[80,896]{1,0:T(8,128)(2,1)S(1)}, u32[]{:S(2)}, u32[]{:S(2)}) %collective-permute-start.20) | collective-permute-done | bytes 143392 | tf_op jit(solution)/shard_map/ppermute | solution.py:750
  67.5 0.7 %add.26 = (bf16[2,32,896]{2,1,0:T(8,128)(2,1)}, bf16[4,4,896]{2,1,0:T(4,128)(2,1)}) custom-call(bf16[80,896]{1,0:T(8,128)(2,1)S(1)} %get-tuple-element.33.refs_0_, bf16[80,896]{1,0:T(8,128)(2,1)S(1)} %collective-permute-done.18.refs_1_, bf16[80,896]{1,0:T(8,128)(2,1)S(1)} %collective-permute-done.19.refs_2_, bf16[80,896]{1,0:T(8,128)(2,1)S(1)} %collective-permute-done.20.refs_3_), custom_call_target="tpu_custom_call" | custom-call | tf_op jit(solution)/shard_map/add/pallas_call | solution.py:754
  (19 shorter events, 0.0 us)
Async XLA Ops:
  0.6 22.5 %collective-permute-start = (bf16[448,896]{1,0:T(8,128)(2,1)}, bf16[448,896]{1,0:T(8,128)(2,1)}, u32[]{:S(2)}, u32[]{:S(2)}) collective-permute-start(bf16[448,896]{1,0:T(8,128)(2,1)} %own_ref.7), channel_id=1, source_target_pairs={{0,4},{4,0},{8,12},{12,8},{16,20},{20,16},{24,28},{28,24},{1,5},{5... | collective-permute-start | bytes 2408456 | tf_op jit(solution)/shard_map/ppermute | solution.py:618
  1.2 42.0 %collective-permute-start.11 = (bf16[448,896]{1,0:T(8,128)(2,1)}, bf16[448,896]{1,0:T(8,128)(2,1)}, u32[]{:S(2)}, u32[]{:S(2)}) collective-permute-start(bf16[448,896]{1,0:T(8,128)(2,1)} %bitcast.20), channel_id=1, source_target_pairs={{0,4},{4,0},{8,12},{12,8},{16,20},{20,16},{24,28},{28,24},{1,5},{5... | collective-permute-start | bytes 2408456 | tf_op jit(solution)/shard_map/ppermute | solution.py:619
  3.5 11.2 %copy-start.11 = (bf16[80,896]{1,0:T(8,128)(2,1)S(1)}, bf16[80,896]{1,0:T(8,128)(2,1)}, u32[]{:S(2)}) copy-start(bf16[80,896]{1,0:T(8,128)(2,1)} %get-tuple-element.17.rest_1_) | copy-start | bytes 430084
  3.5 14.6 %copy-start.10 = (bf16[80,896]{1,0:T(8,128)(2,1)S(1)}, bf16[80,896]{1,0:T(8,128)(2,1)}, u32[]{:S(2)}) copy-start(bf16[80,896]{1,0:T(8,128)(2,1)} %get-tuple-element.18.rest_2_) | copy-start | bytes 430084
  3.5 16.4 %copy-start.9 = (bf16[80,896]{1,0:T(8,128)(2,1)S(1)}, bf16[80,896]{1,0:T(8,128)(2,1)}, u32[]{:S(2)}) copy-start(bf16[80,896]{1,0:T(8,128)(2,1)} %get-tuple-element.19.rest_3_) | copy-start | bytes 430084
  3.6 19.6 %copy-start = (bf16[448,896]{1,0:T(8,128)(2,1)S(1)}, bf16[448,896]{1,0:T(8,128)(2,1)}, u32[]{:S(2)}) copy-start(bf16[448,896]{1,0:T(8,128)(2,1)} %own_ref.7) | copy-start | bytes 2408452
  7.3 7.5 %collective-permute-start.9 = (bf16[384,128]{1,0:T(8,128)(2,1)}, bf16[384,128]{1,0:T(8,128)(2,1)S(1)}, u32[]{:S(2)}, u32[]{:S(2)}) collective-permute-start(bf16[384,128]{1,0:T(8,128)(2,1)} %get-tuple-element.29), channel_id=1, source_target_pairs={{0,24},{4,28},{8,16},{12,20},{16,8},{20,12},{24,0},{28,4},{1,25},{... | collective-permute-start | bytes 294920 | tf_op jit(solution)/shard_map/ppermute | solution.py:596
  11.2 5.6 %collective-permute-start.8 = (bf16[384,128]{1,0:T(8,128)(2,1)}, bf16[384,128]{1,0:T(8,128)(2,1)S(1)}, u32[]{:S(2)}, u32[]{:S(2)}) collective-permute-start(bf16[384,128]{1,0:T(8,128)(2,1)} %get-tuple-element.29), channel_id=1, source_target_pairs={{0,16},{4,20},{8,24},{12,28},{16,0},{20,4},{24,8},{28,12},{1,17},{... | collective-permute-start | bytes 294920 | tf_op jit(solution)/shard_map/ppermute | solution.py:596
  11.7 5.3 %collective-permute-start.7 = (bf16[384,128]{1,0:T(8,128)(2,1)}, bf16[384,128]{1,0:T(8,128)(2,1)S(1)}, u32[]{:S(2)}, u32[]{:S(2)}) collective-permute-start(bf16[384,128]{1,0:T(8,128)(2,1)} %get-tuple-element.29), channel_id=1, source_target_pairs={{0,8},{4,12},{8,0},{12,4},{16,24},{20,28},{24,16},{28,20},{1,9},{5... | collective-permute-start | bytes 294920 | tf_op jit(solution)/shard_map/ppermute | solution.py:596
  14.8 5.1 %collective-permute-start.1 = (bf16[80,896]{1,0:T(8,128)(2,1)S(1)}, bf16[80,896]{1,0:T(8,128)(2,1)S(1)}, u32[]{:S(2)}, u32[]{:S(2)}) collective-permute-start(bf16[80,896]{1,0:T(8,128)(2,1)S(1)} %copy-done.11), channel_id=1, source_target_pairs={{0,8},{4,12},{8,0},{12,4},{16,24},{20,28},{24,16},{28,20},{1,9},{5... | collective-permute-start | bytes 430088 | tf_op jit(solution)/shard_map/ppermute | solution.py:596
  18.0 17.6 %collective-permute-start.10 = (bf16[4,384,128]{2,1,0:T(8,128)(2,1)S(1)}, bf16[4,384,128]{2,1,0:T(8,128)(2,1)S(1)}, u32[]{:S(2)}, u32[]{:S(2)}) collective-permute-start(bf16[4,384,128]{2,1,0:T(8,128)(2,1)S(1)} %pad_maximum_fusion.1.rest_4_), channel_id=1, source_target_pairs={{0,4},{4,0},{8,12},{12,8},{16,20},{20,16},{24,28},{28,24},{1,5},{5... | collective-permute-start | bytes 1179656 | tf_op jit(solution)/shard_map/ppermute | solution.py:654
  18.1 8.9 %collective-permute-start.3 = (bf16[80,896]{1,0:T(8,128)(2,1)S(1)}, bf16[80,896]{1,0:T(8,128)(2,1)S(1)}, u32[]{:S(2)}, u32[]{:S(2)}) collective-permute-start(bf16[80,896]{1,0:T(8,128)(2,1)S(1)} %copy-done.10), channel_id=1, source_target_pairs={{0,16},{4,20},{8,24},{12,28},{16,0},{20,4},{24,8},{28,12},{1,17},{... | collective-permute-start | bytes 430088 | tf_op jit(solution)/shard_map/ppermute | solution.py:596
  19.9 10.5 %collective-permute-start.5 = (bf16[80,896]{1,0:T(8,128)(2,1)S(1)}, bf16[80,896]{1,0:T(8,128)(2,1)S(1)}, u32[]{:S(2)}, u32[]{:S(2)}) collective-permute-start(bf16[80,896]{1,0:T(8,128)(2,1)S(1)} %copy-done.9), channel_id=1, source_target_pairs={{0,24},{4,28},{8,16},{12,20},{16,8},{20,12},{24,0},{28,4},{1,25},{... | collective-permute-start | bytes 430088 | tf_op jit(solution)/shard_map/ppermute | solution.py:596
  24.7 9.1 %copy-start.2 = (bf16[80,896]{1,0:T(8,128)(2,1)S(1)}, bf16[80,896]{1,0:T(8,128)(2,1)}, u32[]{:S(2)}) copy-start(bf16[80,896]{1,0:T(8,128)(2,1)} %get-tuple-element.16.rest_0_.rows_ref) | copy-start | bytes 430084
  24.7 9.1 %copy-start.3 = (f32[80,128]{1,0:T(8,128)S(1)}, f32[80,128]{1,0:T(8,128)}, u32[]{:S(2)}) copy-start(f32[80,128]{1,0:T(8,128)} %get-tuple-element.20.rest_0_) | copy-start | bytes 122884
  24.8 9.1 %copy-start.4 = (f32[80,128]{1,0:T(8,128)S(1)}, f32[80,128]{1,0:T(8,128)}, u32[]{:S(2)}) copy-start(f32[80,128]{1,0:T(8,128)} %get-tuple-element.21.rest_1_) | copy-start | bytes 122884
  24.8 9.1 %copy-start.5 = (bf16[2,16,128]{2,1,0:T(8,128)(2,1)S(1)}, bf16[2,16,128]{2,1,0:T(8,128)(2,1)}, u32[]{:S(2)}) copy-start(bf16[2,16,128]{2,1,0:T(8,128)(2,1)} %get-tuple-element.22.rest_2_) | copy-start | bytes 24580
  24.8 9.1 %copy-start.6 = (f32[896]{0:T(1024)S(1)}, f32[896]{0:T(1024)}, u32[]{:S(2)}) copy-start(f32[896]{0:T(1024)} %bias_ref.1) | copy-start | bytes 10756
  24.8 9.1 %copy-start.7 = (s32[2]{0:T(128)S(1)}, s32[2]{0:T(128)}, u32[]{:S(2)}) copy-start(s32[2]{0:T(128)} %lengths_ref.3) | copy-start | bytes 28
  24.8 9.1 %copy-start.8 = (s32[4]{0:T(128)S(1)}, s32[4]{0:T(128)}, u32[]{:S(2)}) copy-start(s32[4]{0:T(128)} %sample_prompt_ref.3) | copy-start | bytes 52
  24.8 10.8 %collective-permute-start.2 = (bf16[80,896]{1,0:T(8,128)(2,1)S(1)}, bf16[80,896]{1,0:T(8,128)(2,1)S(1)}, u32[]{:S(2)}, u32[]{:S(2)}) collective-permute-start(bf16[80,896]{1,0:T(8,128)(2,1)S(1)} %query_dot.3), channel_id=1, source_target_pairs={{0,8},{4,12},{8,0},{12,4},{16,24},{20,28},{24,16},{28,20},{1,9},{5... | collective-permute-start | bytes 430088 | tf_op jit(solution)/shard_map/ppermute | solution.py:596
  28.6 7.6 %collective-permute-start.4 = (bf16[80,896]{1,0:T(8,128)(2,1)S(1)}, bf16[80,896]{1,0:T(8,128)(2,1)S(1)}, u32[]{:S(2)}, u32[]{:S(2)}) collective-permute-start(bf16[80,896]{1,0:T(8,128)(2,1)S(1)} %query_dot.4), channel_id=1, source_target_pairs={{0,16},{4,20},{8,24},{12,28},{16,0},{20,4},{24,8},{28,12},{1,17},{... | collective-permute-start | bytes 430088 | tf_op jit(solution)/shard_map/ppermute | solution.py:596
  32.0 6.1 %collective-permute-start.6 = (bf16[80,896]{1,0:T(8,128)(2,1)S(1)}, bf16[80,896]{1,0:T(8,128)(2,1)S(1)}, u32[]{:S(2)}, u32[]{:S(2)}) collective-permute-start(bf16[80,896]{1,0:T(8,128)(2,1)S(1)} %query_dot.5), channel_id=1, source_target_pairs={{0,24},{4,28},{8,16},{12,20},{16,8},{20,12},{24,0},{28,4},{1,25},{... | collective-permute-start | bytes 430088 | tf_op jit(solution)/shard_map/ppermute | solution.py:596
  33.9 9.4 %copy-start.1 = (bf16[896,448]{0,1:T(8,128)(2,1)S(1)}, bf16[896,448]{0,1:T(8,128)(2,1)}, u32[]{:S(2)}) copy-start(bf16[896,448]{0,1:T(8,128)(2,1)} %param.25) | copy-start | bytes 2408452
  39.7 6.1 %collective-permute-start.16 = (bf16[80,896]{1,0:T(8,128)(2,1)S(1)}, bf16[80,896]{1,0:T(8,128)(2,1)S(1)}, u32[]{:S(2)}, u32[]{:S(2)}) collective-permute-start(bf16[80,896]{1,0:T(8,128)(2,1)S(1)} %attend.1.rows_ref), channel_id=1, source_target_pairs={{0,24},{4,28},{8,16},{12,20},{16,8},{20,12},{24,0},{28,4},{1,25},{... | collective-permute-start | bytes 430088 | tf_op jit(solution)/shard_map/ppermute | solution.py:596
  41.4 8.1 %collective-permute-start.14 = (bf16[80,896]{1,0:T(8,128)(2,1)S(1)}, bf16[80,896]{1,0:T(8,128)(2,1)S(1)}, u32[]{:S(2)}, u32[]{:S(2)}) collective-permute-start(bf16[80,896]{1,0:T(8,128)(2,1)S(1)} %attend.1.rows_ref), channel_id=1, source_target_pairs={{0,16},{4,20},{8,24},{12,28},{16,0},{20,4},{24,8},{28,12},{1,17},{... | collective-permute-start | bytes 430088 | tf_op jit(solution)/shard_map/ppermute | solution.py:596
  41.9 8.7 %collective-permute-start.12 = (bf16[80,896]{1,0:T(8,128)(2,1)S(1)}, bf16[80,896]{1,0:T(8,128)(2,1)S(1)}, u32[]{:S(2)}, u32[]{:S(2)}) collective-permute-start(bf16[80,896]{1,0:T(8,128)(2,1)S(1)} %attend.1.rows_ref), channel_id=1, source_target_pairs={{0,8},{4,12},{8,0},{12,4},{16,24},{20,28},{24,16},{28,20},{1,9},{5... | collective-permute-start | bytes 430088 | tf_op jit(solution)/shard_map/ppermute | solution.py:596
  46.2 6.8 %collective-permute-start.17 = (bf16[80,896]{1,0:T(8,128)(2,1)S(1)}, bf16[80,896]{1,0:T(8,128)(2,1)S(1)}, u32[]{:S(2)}, u32[]{:S(2)}) collective-permute-start(bf16[80,896]{1,0:T(8,128)(2,1)S(1)} %out_dot.7), channel_id=1, source_target_pairs={{0,24},{4,28},{8,16},{12,20},{16,8},{20,12},{24,0},{28,4},{1,25},{... | collective-permute-start | bytes 430088 | tf_op jit(solution)/shard_map/ppermute | solution.py:596
  49.9 5.2 %collective-permute-start.15 = (bf16[80,896]{1,0:T(8,128)(2,1)S(1)}, bf16[80,896]{1,0:T(8,128)(2,1)S(1)}, u32[]{:S(2)}, u32[]{:S(2)}) collective-permute-start(bf16[80,896]{1,0:T(8,128)(2,1)S(1)} %out_dot.6), channel_id=1, source_target_pairs={{0,16},{4,20},{8,24},{12,28},{16,0},{20,4},{24,8},{28,12},{1,17},{... | collective-permute-start | bytes 430088 | tf_op jit(solution)/shard_map/ppermute | solution.py:596
  51.0 5.2 %collective-permute-start.13 = (bf16[80,896]{1,0:T(8,128)(2,1)S(1)}, bf16[80,896]{1,0:T(8,128)(2,1)S(1)}, u32[]{:S(2)}, u32[]{:S(2)}) collective-permute-start(bf16[80,896]{1,0:T(8,128)(2,1)S(1)} %out_dot.5), channel_id=1, source_target_pairs={{0,8},{4,12},{8,0},{12,4},{16,24},{20,28},{24,16},{28,20},{1,9},{5... | collective-permute-start | bytes 430088 | tf_op jit(solution)/shard_map/ppermute | solution.py:596
  56.4 5.2 %collective-permute-start.18 = (bf16[80,896]{1,0:T(8,128)(2,1)S(1)}, bf16[80,896]{1,0:T(8,128)(2,1)S(1)}, u32[]{:S(2)}, u32[]{:S(2)}) collective-permute-start(bf16[80,896]{1,0:T(8,128)(2,1)S(1)} %get-tuple-element.32), channel_id=1, source_target_pairs={{0,1},{1,0},{2,3},{3,2},{4,5},{5,4},{6,7},{7,6},{8,9},{9,8},{10,11... | collective-permute-start | bytes 430088 | tf_op jit(solution)/shard_map/ppermute | solution.py:750
  57.9 7.5 %collective-permute-start.19 = (bf16[80,896]{1,0:T(8,128)(2,1)S(1)}, bf16[80,896]{1,0:T(8,128)(2,1)S(1)}, u32[]{:S(2)}, u32[]{:S(2)}) collective-permute-start(bf16[80,896]{1,0:T(8,128)(2,1)S(1)} %get-tuple-element.31), channel_id=1, source_target_pairs={{0,2},{1,3},{2,0},{3,1},{4,6},{5,7},{6,4},{7,5},{8,10},{9,11},{10,... | collective-permute-start | bytes 430088 | tf_op jit(solution)/shard_map/ppermute | solution.py:750
  60.5 7.0 %collective-permute-start.20 = (bf16[80,896]{1,0:T(8,128)(2,1)S(1)}, bf16[80,896]{1,0:T(8,128)(2,1)S(1)}, u32[]{:S(2)}, u32[]{:S(2)}) collective-permute-start(bf16[80,896]{1,0:T(8,128)(2,1)S(1)} %get-tuple-element.30), channel_id=1, source_target_pairs={{0,3},{1,2},{2,1},{3,0},{4,7},{5,6},{6,5},{7,4},{8,11},{9,10},{10,... | collective-permute-start | bytes 430088 | tf_op jit(solution)/shard_map/ppermute | solution.py:750
